TPU v7x, 32 devices: a whole 2x2x4 slice. The times are simulated.
32 devices in a mesh: groups: 2 (over x), blk: 16 (over z, y, core).
Axes of the slice: x: 2, y: 2, z: 4, core: 2. Of those that a mesh axis runs over, the one named last changes fastest.
Arguments:
- walkers: bfloat16 [64, 65536], P(('groups', 'blk')), parts along dimension 0, may hold values from -6 to 6
- intersection_inv: bfloat16 [64, 4096], P(('groups', 'blk')), parts along dimension 0, may hold values from -0.75 to 0.75
- new_slot: int32 [64], P(('groups', 'blk')), parts along dimension 0, may hold values from 0 to 31, as said below
- cholesky: bfloat16 [2048, 64, 10240], P(('groups', 'blk')), parts along dimension 0, may hold values from -0.0234375 to 0.0234375
Outputs:
- moved_walkers: bfloat16 [64, 65536], P(('groups', 'blk')), parts along dimension 0
- moved_intersection_inv: bfloat16 [64, 4096], P(('groups', 'blk')), parts along dimension 0
- force_bias: float32 [64, 10240], P(('groups', 'blk')), parts along dimension 0
There are 2 independent parts, one for each index of `groups`. A program takes and returns all parts, laid end to end along the dimension named above; each array names one. Nothing has to cross between parts.
Inputs may be any that keep to these rules, and one draw needn't show every extreme that they name: new_slot is a permutation; the new owner of walker w is new_slot[w] // 2; the 2 walkers of one device go to 2 different owners, and new_slot[w] % 2 == w % 2.
All inputs are finite; a program needn't handle non-finite values.
Results may differ from a plain program's by a relative error of at most 0.0028.
Values may be sent and summed in bfloat16 or wider, within the bound.
No kernel may reach another device: no remote copies, remote signals or barrier semaphores. Data moves between devices by JAX's collectives and lax.ppermute only.
A program may use at most 128 MiB of HBM per device.

v0:
```python
import jax
import jax.numpy as jnp
from jax import lax
from jax.sharding import PartitionSpec as P


def local(walkers, intersection_inv, new_slot, cholesky):
    cycle_size = lax.axis_size("blk")
    my_index = lax.axis_index("blk")
    walk_dev = walkers.shape[0]
    walk_total = walk_dev * cycle_size
    orbit_local = cholesky.shape[0]
    occupied = cholesky.shape[1]
    chol_flat = cholesky.reshape(orbit_local * occupied, cholesky.shape[2])
    all_slots = lax.all_gather(new_slot, "blk", axis=0, tiled=True)
    anchor = (
        jnp.zeros((walk_total,), jnp.int32)
        .at[all_slots]
        .set(jnp.arange(walk_total, dtype=jnp.int32))
    )
    local_orbit = lax.all_to_all(walkers, "blk", split_axis=1, concat_axis=0, tiled=True)
    all_inverse = lax.all_gather(intersection_inv, "blk", axis=0, tiled=True)
    perm_orbit = local_orbit[anchor]
    perm_inverse = all_inverse[anchor]
    greens = jnp.einsum(
        "wpj,wij->wpi",
        perm_orbit.reshape(walk_total, orbit_local, occupied),
        perm_inverse.reshape(walk_total, occupied, occupied),
        preferred_element_type=jnp.float32,
    ).astype(jnp.bfloat16)
    green_orbit = greens.reshape(walk_total, orbit_local * occupied)
    moved_walk = lax.all_to_all(perm_orbit, "blk", split_axis=0, concat_axis=1, tiled=True)
    moved_inverse = lax.dynamic_slice_in_dim(perm_inverse, my_index * walk_dev, walk_dev, 0)
    force_bias = lax.psum_scatter(
        jnp.dot(green_orbit, chol_flat, preferred_element_type=jnp.float32),
        "blk",
        scatter_dimension=0,
        tiled=True,
    )
    return (moved_walk, moved_inverse, force_bias)


def solution(mesh):
    placed = (
        P(("groups", "blk"), None),
        P(("groups", "blk"), None),
        P(("groups", "blk")),
        P(("groups", "blk"), None, None),
    )
    return jax.shard_map(
        local,
        mesh=mesh,
        in_specs=placed,
        out_specs=(
            P(("groups", "blk"), None),
            P(("groups", "blk"), None),
            P(("groups", "blk"), None),
        ),
        check_vma=False,
    )
```

profile of v0, /device:TPU:0, one launch (start us, length us, event | category | flops | bytes accessed | tf_op | source)
XLA Modules:
  0.0 186.7 jit_solution(3166553028669388083)
XLA Ops:
  7.2 7.4 %all-to-all-start = ((bf16[2,16,4096]{2,0,1:T(2,128)(2,1)}), bf16[2,16,4096]{2,0,1:T(2,128)(2,1)S(1)}, u32[]{:S(2)}, u32[]{:S(2)}) async-start(bf16[2,16,4096]{2,0,1:T(2,128)(2,1)} %bitcast.16), calls=%async_computation | async-start | bytes 524288 | tf_op jit(solution)/shard_map/all_to_all | solution.py:21
  14.6 0.0 all-reduce.4.cloned.1.call-start
  14.7 1.3 fusion.2
  16.6 0.9 dynamic-update-slice
  17.5 12.4 %all-reduce = s32[32]{0:T(128)S(1)} all-reduce(s32[32]{0:T(128)S(1)} %dynamic-update-slice), channel_id=1, replica_groups=mesh['groups'=2,'blk'=16] {'blk'}, use_global_device_ids=true, to_apply=%add | all-reduce | flops 32 | bytes 256
  29.9 18.9 %all-gather = bf16[16,2,4096]{2,1,0:T(2,128)(2,1)S(1)} all-gather(bf16[1,2,4096]{2,1,0:T(2,128)(2,1)} %bitcast.17), channel_id=1, replica_groups=mesh['groups'=2,'blk'=16] {'blk'}, dimensions={0}, use_global_device_ids=true | all-gather | bytes 278528 | tf_op jit(solution)/shard_map/all_gather | solution.py:22
  48.8 0.1 reshape.53
  48.9 0.7 scatter_custom_fusion
  49.6 0.7 gather_fusion.1
  50.3 0.5 reshape.21
  50.9 0.0 all-to-all-done
  50.9 0.1 all_to_all.31
  51.0 0.7 gather_fusion
  51.7 0.5 reshape.20
  52.2 0.4 fusion.3
  52.6 30.0 %convolution_bitcast_fusion = f32[32,10240]{1,0:T(8,128)} fusion(bf16[64,64,10240]{2,1,0:T(8,128)(2,1)} %param.7, bf16[32,64,64]{2,1,0:T(8,128)(2,1)S(1)} %fusion.3), kind=kOutput, calls=%fused_computation.3 | convolution fusion | flops 2684354560 | bytes 85458944 | tf_op jit(solution)/shard_map/dot_general | solution.py:35
  82.7 0.0 all-reduce.4.cloned.1.call-update
  82.7 0.9 all_to_all.32
  83.6 3.5 %all-to-all-start.1 = ((bf16[16,2,4096]{2,1,0:T(2,128)(2,1)}), bf16[16,2,4096]{2,1,0:T(2,128)(2,1)S(1)}, u32[]{:S(2)}, u32[]{:S(2)}) async-start(bf16[16,2,4096]{2,1,0:T(2,128)(2,1)} %all_to_all.32), calls=%async_computation.1 | async-start | bytes 524288 | tf_op jit(solution)/shard_map/all_to_all | solution.py:32
  87.8 0.6 constant_dynamic-slice_fusion.1
  88.4 10.8 %all-to-all-done.1 = bf16[16,2,4096]{2,1,0:T(2,128)(2,1)S(1)} async-done(((bf16[16,2,4096]{2,1,0:T(2,128)(2,1)}), bf16[16,2,4096]{2,1,0:T(2,128)(2,1)S(1)}, u32[]{:S(2)}, u32[]{:S(2)}) %all-to-all-start.1) | async-done | bytes 262176 | tf_op jit(solution)/shard_map/all_to_all | solution.py:32
  99.2 78.3 %all-reduce.4.cloned.1.call-done = f32[32,10240]{1,0:T(8,128)} async-done(((f32[32,10240]{1,0:T(8,128)}), f32[32,10240]{1,0:T(8,128)}) %all-reduce.4.cloned.1.call-update) | async-done | bytes 1310736
  177.5 1.6 constant_dynamic-slice_fusion
  179.2 0.7 copy.17
  (5 shorter events, 0.0 us)
Async XLA Ops:
  7.2 43.7 %all-to-all-start = ((bf16[2,16,4096]{2,0,1:T(2,128)(2,1)}), bf16[2,16,4096]{2,0,1:T(2,128)(2,1)S(1)}, u32[]{:S(2)}, u32[]{:S(2)}) async-start(bf16[2,16,4096]{2,0,1:T(2,128)(2,1)} %bitcast.16), calls=%async_computation | async-start | bytes 524288 | tf_op jit(solution)/shard_map/all_to_all | solution.py:21
  14.6 162.9 %all-reduce.4.cloned.1.call-start = ((), (), s32[]{:S(2)}) async-start(), calls=%async_computation.2 | async-start | bytes 2621440
  83.6 15.7 %all-to-all-start.1 = ((bf16[16,2,4096]{2,1,0:T(2,128)(2,1)}), bf16[16,2,4096]{2,1,0:T(2,128)(2,1)S(1)}, u32[]{:S(2)}, u32[]{:S(2)}) async-start(bf16[16,2,4096]{2,1,0:T(2,128)(2,1)} %all_to_all.32), calls=%async_computation.1 | async-start | bytes 524288 | tf_op jit(solution)/shard_map/all_to_all | solution.py:32
Sparse Core Ops, SparseCore 0:
  82.8 94.7 all-reduce.3
where the time goes:
time: 187 us
  waiting for transfers between devices  89.2 us (48%)
  blocking collectives  31.3 us (17%)
  matrix products  30.4 us (16%)
  between operations  15.5 us (8%)
  starting transfers between devices  11 us (6%)
  local copies, waits for them, and re-layouts  9.4 us (5%)
    unnamed x2, waiting for transfers between devices  78.3 us
    dot_general x1, matrix products, local(): jnp.dot(green_orbit, chol_flat, preferred_element_type=jnp.float32)  30 us
    all_gather x1, blocking collectives, local(): all_inverse = lax.all_gather(intersection_inv, 'blk', axis=0, tiled=True)  18.9 us
    unnamed x1, blocking collectives  12.4 us
    all_to_all x1, waiting for transfers between devices, local(): lax.all_to_all(perm_orbit, 'blk', split_axis=0, concat_axis=1, tiled=True)  10.8 us
    all_to_all x1, starting transfers between devices, local(): lax.all_to_all(walkers, 'blk', split_axis=1, concat_axis=0, tiled=True)  7.43 us
    unnamed x5, local copies, waits for them, and re-layouts  4.62 us
  transfers between devices with their start and end apart: 3, of which 2 were waited for; matrix products, arithmetic and copies ran while one was open for 3% of the time, Pallas kernels for 0%

commit v1 on v0

v1 whole, which is shorter than its diff:
```python
import jax
import jax.numpy as jnp
from jax import lax
from jax.experimental import pallas as pl
from jax.experimental.pallas import tpu as pltpu
from jax.sharding import PartitionSpec as P


BF = jnp.bfloat16
F32 = jnp.float32
LANES = 128
SLOT_ROWS = 4
RADIX = 256


def greens_kernel(slot_ref, walk_ref, inv_ref, share_ref, out_ref):
    devices = out_ref.shape[0]
    walk_dev, all_rows, _ = walk_ref.shape
    rows = all_rows // devices
    base = 2 * walk_dev * rows
    for w in range(walk_dev):
        inv = inv_ref[w]
        zero = jnp.zeros_like(inv)
        both = jnp.concatenate(
            [jnp.concatenate([inv, zero], 1), jnp.concatenate([zero, inv], 1)], 0
        )
        coefficients = walk_ref[w]
        greens = lax.dot_general(
            coefficients, both, (((1,), (1,)), ((), ())), preferred_element_type=F32
        ).astype(BF)
        for d in range(devices):
            piece = slice(d * rows, (d + 1) * rows)
            out_ref[d, w * rows : (w + 1) * rows, :] = greens[piece]
            at = (walk_dev + w) * rows
            out_ref[d, at : at + rows, :] = coefficients[piece]
    row = lax.broadcasted_iota(jnp.int32, (SLOT_ROWS, LANES), 0)
    lane = lax.broadcasted_iota(jnp.int32, (SLOT_ROWS, LANES), 1)
    tail = jnp.zeros((SLOT_ROWS, LANES), F32)
    for w in range(walk_dev):
        slot = slot_ref[w]
        low = jnp.broadcast_to(slot % RADIX, tail.shape).astype(F32)
        high = jnp.broadcast_to(slot // RADIX, tail.shape).astype(F32)
        here = lane == w
        tail = jnp.where(here & (row == 0), low, tail)
        tail = jnp.where(here & (row == 1), high, tail)
    for d in range(devices):
        out_ref[d, base : base + SLOT_ROWS, :] = tail.astype(BF)
        out_ref[d, base + SLOT_ROWS :, :] = share_ref[d]


def sort_kernel(core_ref, got_ref, green_ref, moved_ref, spread, seats, seat_smem, sem):
    devices, width, _ = got_ref.shape
    total, contract = green_ref.shape
    walk_dev = total // devices
    rows = contract // LANES
    base = 2 * walk_dev * rows
    share_rows = width - base - SLOT_ROWS
    each = share_rows // walk_dev
    core = core_ref[0]
    for d in range(devices):
        seats[d : d + 1, :] = (
            got_ref[d, base : base + 1, :].astype(F32)
            + RADIX * got_ref[d, base + 1 : base + 2, :].astype(F32)
        ).astype(jnp.int32)
    copy = pltpu.make_async_copy(seats, seat_smem, sem)
    copy.start()
    copy.wait()
    for d in range(devices):
        for w in range(walk_dev):
            slot = seat_smem[d, w]
            owner = slot // walk_dev
            side = jnp.where(owner % 2 == core, total // 2, 0)
            seat = side + (owner // 2) * walk_dev + w
            spread[pl.ds(seat, rows, stride=total), :] = got_ref[
                d, w * rows : (w + 1) * rows, :
            ].astype(F32)
            at = (walk_dev + w) * rows
            moved_ref[owner, w * rows : (w + 1) * rows, :] = got_ref[d, at : at + rows, :]
            tail = walk_dev * rows + w * each
            at = base + SLOT_ROWS + w * each
            moved_ref[owner, tail : tail + each, :] = got_ref[d, at : at + each, :]
    for r in range(rows):
        green_ref[:, r * LANES : (r + 1) * LANES] = spread[
            r * total : (r + 1) * total, :
        ].astype(BF)


def bias_kernel(green_ref, chol_ref, send_ref, keep_ref, buf, sem):
    slots, step, _ = buf.shape
    half = send_ref.shape[0]
    count = chol_ref.shape[0] // step

    def copy(i):
        return pltpu.make_async_copy(
            chol_ref.at[pl.ds(i * step, step)], buf.at[i % slots], sem.at[i % slots]
        )

    for i in range(min(slots, count)):
        copy(i).start()
    for i in range(count):
        copy(i).wait()
        part = jnp.dot(
            green_ref[:, i * step : (i + 1) * step],
            buf[i % slots],
            preferred_element_type=F32,
        )
        if i == 0:
            send_ref[...] = part[:half]
            keep_ref[...] = part[half:]
        else:
            send_ref[...] += part[:half]
            keep_ref[...] += part[half:]
        if i + slots < count:
            copy(i + slots).start()


def local(walkers, intersection_inv, new_slot, cholesky):
    devices = lax.axis_size("blk")
    me = lax.axis_index("blk")
    walk_dev = walkers.shape[0]
    total = walk_dev * devices
    occupied = cholesky.shape[1]
    contract = cholesky.shape[0] * occupied
    vectors = cholesky.shape[2]
    rows = contract // LANES
    chips = devices // 2
    chol = cholesky.reshape(contract, vectors)

    share = intersection_inv.shape[1] // devices
    share_pad = -share % LANES
    share_rows = walk_dev * (share + share_pad) // LANES
    width = 2 * walk_dev * rows + SLOT_ROWS + share_rows
    vmem = pl.BlockSpec(memory_space=pltpu.VMEM)
    smem = pl.BlockSpec(memory_space=pltpu.SMEM)
    hbm = pl.BlockSpec(memory_space=pl.ANY)

    packed = pl.pallas_call(
        greens_kernel,
        in_specs=[smem, vmem, vmem, vmem],
        out_specs=vmem,
        out_shape=jax.ShapeDtypeStruct((devices, width, LANES), BF),
    )(
        new_slot,
        walkers.reshape(walk_dev, devices * rows, LANES),
        intersection_inv.reshape(walk_dev, occupied, occupied),
        jnp.pad(
            intersection_inv.reshape(walk_dev, devices, share), ((0, 0), (0, 0), (0, share_pad))
        )
        .transpose(1, 0, 2)
        .reshape(devices, share_rows, LANES),
    )
    got = lax.all_to_all(packed, "blk", split_axis=0, concat_axis=0, tiled=True)

    greens, back = pl.pallas_call(
        sort_kernel,
        in_specs=[smem, vmem],
        out_specs=[vmem, vmem],
        out_shape=[
            jax.ShapeDtypeStruct((total, contract), BF),
            jax.ShapeDtypeStruct((devices, walk_dev * rows + share_rows, LANES), BF),
        ],
        scratch_shapes=[
            pltpu.VMEM((rows * total, LANES), F32),
            pltpu.VMEM((devices, LANES), jnp.int32),
            pltpu.SMEM((devices, LANES), jnp.int32),
            pltpu.SemaphoreType.DMA,
        ],
        compiler_params=pltpu.CompilerParams(vmem_limit_bytes=4 << 20),
    )((me % 2).reshape(1).astype(jnp.int32), got)

    moved = lax.all_to_all(back, "blk", split_axis=0, concat_axis=0, tiled=True)
    moved_walk = (
        moved[:, : walk_dev * rows]
        .reshape(devices, walk_dev, rows, LANES)
        .transpose(1, 0, 2, 3)
        .reshape(walk_dev, devices * contract)
    )
    moved_inverse = (
        moved[:, walk_dev * rows :]
        .reshape(devices, walk_dev, share + share_pad)[:, :, :share]
        .transpose(1, 0, 2)
        .reshape(walk_dev, devices * share)
    )

    half = total // 2
    step = min(LANES, contract // 4)
    ring = min(12, contract // step)
    bias_call = pl.pallas_call(
        bias_kernel,
        in_specs=[vmem, hbm],
        out_specs=[vmem, vmem],
        out_shape=[jax.ShapeDtypeStruct((half, vectors), F32)] * 2,
        scratch_shapes=[
            pltpu.VMEM((ring, step, vectors), BF),
            pltpu.SemaphoreType.DMA((ring,)),
        ],
        compiler_params=pltpu.CompilerParams(
            vmem_limit_bytes=ring * step * vectors * 2 + half * vectors * 8 + (4 << 20)
        ),
        cost_estimate=pl.CostEstimate(
            flops=60_000_000_000, bytes_accessed=contract * vectors * 2, transcendentals=0
        ),
    )
    send, keep = bias_call(greens, chol)

    pairs = [(i, i ^ 1) for i in range(devices)]
    both = keep + lax.ppermute(send, "blk", pairs)
    parts = both.astype(BF).reshape(chips, walk_dev, vectors)
    parity = [[2 * c + p for c in range(chips)] for p in range(2)]
    parts = lax.all_to_all(
        parts, "blk", split_axis=0, concat_axis=0, tiled=True, axis_index_groups=parity
    )
    bias = jnp.sum(parts.astype(F32), axis=0)
    return moved_walk, moved_inverse, bias


def solution(mesh):
    spec = P(("groups", "blk"), None)
    return jax.shard_map(
        local,
        mesh=mesh,
        in_specs=(spec, spec, P(("groups", "blk")), P(("groups", "blk"), None, None)),
        out_specs=(spec, spec, spec),
        check_vma=False,
    )
```

time: 187 us -> 88.2 us (0.47)
  waiting for transfers between devices: 89.2 us -> 33.4 us
  blocking collectives: 31.3 us -> 0 us
  matrix products: 30.4 us -> 0 us
  Pallas kernels: 0 us -> 29.8 us
  between operations: 15.5 us -> 0.72 us
  starting transfers between devices: 11 us -> 15.6 us
  local copies, waits for them, and re-layouts: 9.4 us -> 7.05 us
    unnamed x2 -> x0, waiting for transfers between devices: 78.3 us -> none
    dot_general x2 -> x0, matrix products: 30.4 us -> none  [the longest x1 30 us: local(): jnp.dot(green_orbit, chol_flat, preferred_element_type=jnp.float32)]
    pallas_call x0 -> x3, Pallas kernels: none -> 29.8 us  [the longest x1 25.8 us: local(): send, keep = bias_call(greens, chol)]
    all_to_all x2 -> x3, waiting for transfers between devices: 10.8 us -> 33.4 us  [the longest x1 14.8 us: local(): got = lax.all_to_all(packed, 'blk', split_axis=0, concat_axis=0, tiled=True)]
    all_gather x1 -> x0, blocking collectives: 18.9 us -> none  [local(): all_inverse = lax.all_gather(intersection_inv, 'blk', axis=0, tiled=True)]
    unnamed x1 -> x0, blocking collectives: 12.4 us -> none
    all_to_all x2 -> x3, starting transfers between devices: 11 us -> 15.4 us  [the longest x1 7.41 us: local(): got = lax.all_to_all(packed, 'blk', split_axis=0, concat_axis=0, tiled=True)]
    reshape x2 -> x4, local copies, waits for them, and re-layouts: 1.07 us -> 4.35 us  [the longest x1 1.43 us: local(): intersection_inv.reshape(walk_dev, occupied, occupied)]
  transfers between devices with their start and end apart: 3 -> 4, of which waited for: 2 -> 3; matrix products, arithmetic and copies ran while one was open for 3% -> 3% of each run, Pallas kernels for 0% -> 0%
where the time goes in v1:
time: 88.2 us; the launch traced here: 87.6 us
  waiting for transfers between devices  33.4 us (38%)
  Pallas kernels  29.8 us (34%)
  starting transfers between devices  15.6 us (18%)
  local copies, waits for them, and re-layouts  7.05 us (8%)
  other arithmetic  0.98 us (1%)
    pallas_call x1, Pallas kernels, local(): send, keep = bias_call(greens, chol)  25.8 us
    all_to_all x1, waiting for transfers between devices, local(): got = lax.all_to_all(packed, 'blk', split_axis=0, concat_axis=0, tiled=True)  14.8 us
    all_to_all x1, waiting for transfers between devices, local(): moved = lax.all_to_all(back, 'blk', split_axis=0, concat_axis=0, tiled=True)  9.5 us
    all_to_all x1, waiting for transfers between devices, local(): lax.all_to_all(parts, 'blk', split_axis=0, concat_axis=0, tiled=True, axi...  9.09 us
    all_to_all x1, starting transfers between devices, local(): got = lax.all_to_all(packed, 'blk', split_axis=0, concat_axis=0, tiled=True)  7.41 us
    all_to_all x1, starting transfers between devices, local(): moved = lax.all_to_all(back, 'blk', split_axis=0, concat_axis=0, tiled=True)  4.54 us
    all_to_all x1, starting transfers between devices, local(): lax.all_to_all(parts, 'blk', split_axis=0, concat_axis=0, tiled=True, axi...  3.43 us
    unnamed x2, local copies, waits for them, and re-layouts  2.66 us
  transfers between devices with their start and end apart: 4, of which 3 were waited for; matrix products, arithmetic and copies ran while one was open for 3% of the time, Pallas kernels for 0%

profile of v1, /device:TPU:0, one launch (start us, length us, event | category | flops | bytes accessed | tf_op | source)
XLA Modules:
  0.0 87.6 jit_solution(1472765753021156495)
XLA Ops:
  0.6 1.4 %reshape.41.inv_ref = bf16[2,64,64]{2,1,0:T(8,128)(2,1)} reshape(bf16[2,4096]{1,0:T(2,128)(2,1)} %param.5) | data formatting | bytes 32768 | tf_op jit(solution)/shard_map/reshape | solution.py:145
  2.1 1.3 %reshape.43.share_ref = bf16[16,4,128]{2,1,0:T(4,128)(2,1)} reshape(bf16[16,2,256]{2,1,0:T(2,128)(2,1)} %bitcast.25) | data formatting | bytes 32768 | tf_op jit(solution)/shard_map/reshape | solution.py:150
  3.4 1.7 %copy.15 = bf16[1,2,512,128]{3,2,1,0:T(8,128)(2,1)} copy(bf16[1,2,512,128]{3,1,2,0:T(2,128)(2,1)} %bitcast.23) | data formatting | bytes 524288
  5.1 2.1 %shard_map.67 = bf16[16,136,128]{2,1,0:T(8,128)(2,1)} custom-call(s32[2]{0:T(128)} %slot_ref.1, bf16[2,512,128]{2,1,0:T(8,128)(2,1)} %bitcast.20, bf16[2,64,64]{2,1,0:T(8,128)(2,1)} %reshape.41.inv_ref, bf16[16,4,128]{2,1,0:T(4,128)(2,1)} %reshape.43.share_ref), custom_call_target="tpu_custom_call" | custom-call | tf_op jit(solution)/shard_map/pallas_call | solution.py:137
  7.2 7.4 %all-to-all-start = ((bf16[16,136,128]{2,1,0:T(8,128)(2,1)}), bf16[16,136,128]{2,1,0:T(8,128)(2,1)S(1)}, u32[]{:S(2)}, u32[]{:S(2)}) async-start(bf16[16,136,128]{2,1,0:T(8,128)(2,1)} %shard_map.67), calls=%async_computation | async-start | bytes 1114112 | tf_op jit(solution)/shard_map/all_to_all | solution.py:152
  14.6 14.8 %all-to-all-done.got_ref = bf16[16,136,128]{2,1,0:T(8,128)(2,1)S(1)} async-done(((bf16[16,136,128]{2,1,0:T(8,128)(2,1)}), bf16[16,136,128]{2,1,0:T(8,128)(2,1)S(1)}, u32[]{:S(2)}, u32[]{:S(2)}) %all-to-all-start) | async-done | bytes 557088 | tf_op jit(solution)/shard_map/all_to_all | solution.py:152
  29.4 2.0 %shard_map.68 = (bf16[32,4096]{1,0:T(8,128)(2,1)S(1)}, bf16[16,68,128]{2,1,0:T(8,128)(2,1)}) custom-call(s32[1]{0:T(128)} %bitcast.core_ref, bf16[16,136,128]{2,1,0:T(8,128)(2,1)S(1)} %all-to-all-done.got_ref), custom_call_target="tpu_custom_call" | custom-call | tf_op jit(solution)/shard_map/pallas_call | solution.py:154
  31.4 25.8 %shard_map.69 = (f32[16,10240]{1,0:T(8,128)S(1)}, f32[16,10240]{1,0:T(8,128)S(1)}) custom-call(bf16[32,4096]{1,0:T(8,128)(2,1)S(1)} %get-tuple-element.8.green_ref, bf16[4096,10240]{1,0:T(8,128)(2,1)} %bitcast.7.chol_ref), custom_call_target="tpu_custom_call" | custom-call | flops 60000002048 | bytes 83886080 | tf_op jit(solution)/shard_map/pallas_call | solution.py:204
  57.2 0.2 collective-permute-start
  57.4 4.5 %all-to-all-start.1 = ((bf16[16,68,128]{2,1,0:T(8,128)(2,1)}), bf16[16,68,128]{2,1,0:T(8,128)(2,1)S(1)}, u32[]{:S(2)}, u32[]{:S(2)}) async-start(bf16[16,68,128]{2,1,0:T(8,128)(2,1)} %get-tuple-element.7), calls=%async_computation.1 | async-start | bytes 589824 | tf_op jit(solution)/shard_map/all_to_all | solution.py:171
  62.0 0.0 collective-permute-done
  62.0 0.1 add_convert_fusion
  62.1 1.0 %reshape.49 = bf16[8,2,10240]{2,1,0:T(2,128)(2,1)} reshape(bf16[16,10240]{1,0:T(8,128)(2,1)S(1)} %add_convert_fusion) | data formatting | bytes 655360 | tf_op jit(solution)/shard_map/reshape | solution.py:208
  63.0 9.5 %all-to-all-done.1 = bf16[16,68,128]{2,1,0:T(8,128)(2,1)S(1)} async-done(((bf16[16,68,128]{2,1,0:T(8,128)(2,1)}), bf16[16,68,128]{2,1,0:T(8,128)(2,1)S(1)}, u32[]{:S(2)}, u32[]{:S(2)}) %all-to-all-start.1) | async-done | bytes 278560 | tf_op jit(solution)/shard_map/all_to_all | solution.py:171
  72.5 3.4 %all-to-all-start.2 = ((bf16[8,2,10240]{2,1,0:T(2,128)(2,1)}), bf16[8,2,10240]{2,1,0:T(2,128)(2,1)S(1)}, u32[]{:S(2)}, u32[]{:S(2)}) async-start(bf16[8,2,10240]{2,1,0:T(2,128)(2,1)} %reshape.49), calls=%async_computation.2 | async-start | bytes 655360 | tf_op jit(solution)/shard_map/all_to_all | solution.py:210
  76.0 1.0 %copy.14 = bf16[1,2,512,128]{3,1,2,0:T(2,128)(2,1)} copy(bf16[1,2,512,128]{3,2,1,0:T(8,128)(2,1)S(1)} %bitcast.21) | data formatting | bytes 524288
  77.0 0.6 reshape.46
  77.6 9.1 %all-to-all-done.2 = bf16[8,2,10240]{2,1,0:T(2,128)(2,1)S(1)} async-done(((bf16[8,2,10240]{2,1,0:T(2,128)(2,1)}), bf16[8,2,10240]{2,1,0:T(2,128)(2,1)S(1)}, u32[]{:S(2)}, u32[]{:S(2)}) %all-to-all-start.2) | async-done | bytes 327712 | tf_op jit(solution)/shard_map/all_to_all | solution.py:210
  86.7 0.9 %convert_reduce_fusion = f32[2,10240]{1,0:T(2,128)} fusion(bf16[8,2,10240]{2,1,0:T(2,128)(2,1)S(1)} %all-to-all-done.2), kind=kLoop, calls=%fused_computation | loop fusion | flops 307200 | bytes 409600 | tf_op jit(solution)/shard_map/reduce_sum | solution.py:213
  (3 shorter events, 0.0 us)
Async XLA Ops:
  7.2 22.2 %all-to-all-start = ((bf16[16,136,128]{2,1,0:T(8,128)(2,1)}), bf16[16,136,128]{2,1,0:T(8,128)(2,1)S(1)}, u32[]{:S(2)}, u32[]{:S(2)}) async-start(bf16[16,136,128]{2,1,0:T(8,128)(2,1)} %shard_map.67), calls=%async_computation | async-start | bytes 1114112 | tf_op jit(solution)/shard_map/all_to_all | solution.py:152
  57.2 4.8 %collective-permute-start = (f32[16,10240]{1,0:T(8,128)S(1)}, f32[16,10240]{1,0:T(8,128)S(1)}, u32[]{:S(2)}, u32[]{:S(2)}) collective-permute-start(f32[16,10240]{1,0:T(8,128)S(1)} %get-tuple-element.10), channel_id=1, source_target_pairs={{0,1},{1,0},{2,3},{3,2},{4,5},{5,4},{6,7},{7,6},{8,9},{9,8},{10,11... | collective-permute-start | bytes 1966088 | tf_op jit(solution)/shard_map/ppermute | solution.py:207
  57.4 15.1 %all-to-all-start.1 = ((bf16[16,68,128]{2,1,0:T(8,128)(2,1)}), bf16[16,68,128]{2,1,0:T(8,128)(2,1)S(1)}, u32[]{:S(2)}, u32[]{:S(2)}) async-start(bf16[16,68,128]{2,1,0:T(8,128)(2,1)} %get-tuple-element.7), calls=%async_computation.1 | async-start | bytes 589824 | tf_op jit(solution)/shard_map/all_to_all | solution.py:171
  72.5 14.2 %all-to-all-start.2 = ((bf16[8,2,10240]{2,1,0:T(2,128)(2,1)}), bf16[8,2,10240]{2,1,0:T(2,128)(2,1)S(1)}, u32[]{:S(2)}, u32[]{:S(2)}) async-start(bf16[8,2,10240]{2,1,0:T(2,128)(2,1)} %reshape.49), calls=%async_computation.2 | async-start | bytes 655360 | tf_op jit(solution)/shard_map/all_to_all | solution.py:210

commit v2 on v0

v2 whole, which is shorter than its diff:
```python
import jax
import jax.numpy as jnp
from jax import lax
from jax.experimental import pallas as pl
from jax.experimental.pallas import tpu as pltpu
from jax.sharding import PartitionSpec as P


BF = jnp.bfloat16
F32 = jnp.float32
LANES = 128
SLOT_ROWS = 8
RADIX = 256
CORES = 2
DIRECT_CHIPS = 8


def target_chip(k, chips):
    if chips <= DIRECT_CHIPS:
        return lax.rem(lax.axis_index("blk") // CORES + k, chips)
    return k


def exchange(messages, chips):
    if chips > DIRECT_CHIPS:
        groups = [[CORES * c + p for c in range(chips)] for p in range(CORES)]
        got = lax.all_to_all(
            jnp.stack(messages),
            "blk",
            split_axis=0,
            concat_axis=0,
            tiled=True,
            axis_index_groups=groups,
        )
        return [got[k] for k in range(chips)]
    got = [messages[0]]
    for k in range(1, chips):
        pairs = [
            (i, (i // CORES + k) % chips * CORES + i % CORES) for i in range(chips * CORES)
        ]
        got.append(lax.ppermute(messages[k], "blk", pairs))
    return got


def pack_kernel(mine_ref, theirs_ref, *refs):
    *out_refs, inverse = refs
    chips = len(out_refs)
    devices = chips * CORES
    walk_dev, blocks, rows, _ = mine_ref.shape
    inv_rows = inverse.shape[0] // (CORES * walk_dev)
    inv_blocks = blocks - devices - 1
    per = LANES * inv_rows
    occupied = int(round(per**0.5))
    group = LANES // occupied
    share = -(-inv_rows // devices)
    walkers = CORES * walk_dev
    base = 2 * walkers * rows
    core = lax.rem(lax.axis_index("blk"), CORES)
    targets = [CORES * target_chip(k, chips) + core for k in range(chips)]
    new_row = lax.broadcasted_iota(jnp.int32, (occupied, occupied), 0)
    old_row = lax.broadcasted_iota(jnp.int32, (occupied, occupied), 1)
    order = (
        old_row == lax.rem(new_row, group) * (occupied // group) + lax.div(new_row, group)
    ).astype(BF)
    row = lax.broadcasted_iota(jnp.int32, (SLOT_ROWS, LANES), 0)
    lane = lax.broadcasted_iota(jnp.int32, (SLOT_ROWS, LANES), 1)
    tail = jnp.zeros((SLOT_ROWS, LANES), F32)
    for n in range(walkers):
        ref, w = (mine_ref, n) if n < walk_dev else (theirs_ref, n - walk_dev)
        flat = jnp.concatenate([ref[w, devices + b] for b in range(inv_blocks)], 0)
        inverse[n * inv_rows : (n + 1) * inv_rows, :] = flat.astype(F32)
        apart = jnp.concatenate(
            [flat[:, a * occupied : (a + 1) * occupied] for a in range(group)], 0
        )
        inv = jnp.dot(order, apart, preferred_element_type=F32).astype(BF)
        zero = jnp.zeros_like(inv)
        both = jnp.concatenate(
            [
                jnp.concatenate([inv if a == b else zero for b in range(group)], 1)
                for a in range(group)
            ],
            0,
        )
        coefficients = jnp.concatenate([ref[w, t] for t in targets], 0)
        greens = lax.dot_general(
            coefficients, both, (((1,), (1,)), ((), ())), preferred_element_type=F32
        ).astype(BF)
        for k in range(chips):
            piece = slice(k * rows, (k + 1) * rows)
            out_refs[k][n * rows : (n + 1) * rows, :] = greens[piece]
            at = (walkers + n) * rows
            out_refs[k][at : at + rows, :] = coefficients[piece]
        numbers = ref[w, blocks - 1].astype(F32)
        tail = jnp.where((lane == n) & (row == 0), numbers[0:1], tail)
        tail = jnp.where((lane == n) & (row == 1), numbers[1:2], tail)
    for k in range(chips):
        out_refs[k][base : base + SLOT_ROWS, :] = tail.astype(BF)
        first = jnp.minimum(targets[k] * share, inv_rows - share)
        for n in range(walkers):
            at = base + SLOT_ROWS + n * share
            out_refs[k][at : at + share, :] = inverse[
                pl.ds(n * inv_rows + first, share), :
            ].astype(BF)


def sort_kernel(*refs):
    *got_refs, green_ref, back_ref, spread, seats, seat_smem, sem = refs
    chips = len(got_refs)
    devices, back_rows, _ = back_ref.shape
    total, contract = green_ref.shape
    walk_dev = total // devices
    walkers = CORES * walk_dev
    rows = contract // LANES
    share = back_rows // walk_dev - rows
    base = 2 * walkers * rows
    core = lax.rem(lax.axis_index("blk"), CORES)
    for m in range(chips):
        low = got_refs[m][base : base + 1, :].astype(F32)
        high = got_refs[m][base + 1 : base + 2, :].astype(F32)
        seats[m : m + 1, :] = (low + RADIX * high).astype(jnp.int32)
    copy = pltpu.make_async_copy(seats, seat_smem, sem)
    copy.start()
    copy.wait()
    for m in range(chips):
        for n in range(walkers):
            w = n % walk_dev
            owner = lax.div(seat_smem[m, n], walk_dev)
            side = jnp.where(lax.rem(owner, CORES) == core, total // 2, 0)
            seat = side + lax.div(owner, CORES) * walk_dev + w
            spread[pl.ds(seat, rows, stride=total), :] = got_refs[m][
                n * rows : (n + 1) * rows, :
            ].astype(F32)
            at = (walkers + n) * rows
            back_ref[owner, w * rows : (w + 1) * rows, :] = got_refs[m][at : at + rows, :]
            tail = walk_dev * rows + w * share
            at = base + SLOT_ROWS + n * share
            back_ref[owner, tail : tail + share, :] = got_refs[m][at : at + share, :]
    for r in range(rows):
        green_ref[:, r * LANES : (r + 1) * LANES] = spread[
            r * total : (r + 1) * total, :
        ].astype(BF)


def prefetch_kernel(chol_ref, out_ref, sem):
    pieces = sem.shape[0]
    size = out_ref.shape[0] // pieces
    copies = [
        pltpu.make_async_copy(
            chol_ref.at[pl.ds(q * size, size)], out_ref.at[pl.ds(q * size, size)], sem.at[q]
        )
        for q in range(pieces)
    ]
    for copy in copies:
        copy.start()
    for copy in copies:
        copy.wait()


def bias_kernel(green_ref, early_ref, chol_ref, send_ref, keep_ref, buf, sem):
    early = early_ref.shape[0]
    slots, step, _ = buf.shape
    half = send_ref.shape[0]
    count = (chol_ref.shape[0] - early) // step

    def copy(i):
        return pltpu.make_async_copy(
            chol_ref.at[pl.ds(early + i * step, step)], buf.at[i % slots], sem.at[i % slots]
        )

    for i in range(min(slots, count)):
        copy(i).start()
    part = jnp.dot(green_ref[:, :early], early_ref[...], preferred_element_type=F32)
    send_ref[...] = part[:half]
    keep_ref[...] = part[half:]
    for i in range(count):
        copy(i).wait()
        part = jnp.dot(
            green_ref[:, early + i * step : early + (i + 1) * step],
            buf[i % slots],
            preferred_element_type=F32,
        )
        send_ref[...] += part[:half]
        keep_ref[...] += part[half:]
        if i + slots < count:
            copy(i + slots).start()


def fold_kernel(keep_ref, got_ref, *refs):
    *out_refs, spread = refs
    chips = len(out_refs)
    half, vectors = keep_ref.shape
    lines = vectors // LANES
    walk_dev = half // chips
    for j in range(lines):
        at = slice(j * LANES, (j + 1) * LANES)
        spread[pl.ds(j, half, stride=lines), :] = keep_ref[:, at] + got_ref[:, at]
    for k in range(chips):
        first = target_chip(k, chips) * (walk_dev * lines)
        if not isinstance(first, int):
            first = pl.multiple_of(first, 8)
        out_refs[k][...] = spread[pl.ds(first, walk_dev * lines), :].astype(BF)


def sum_kernel(*refs):
    *got_refs, out_ref, spread = refs
    total = got_refs[0][...].astype(F32)
    for ref in got_refs[1:]:
        total = total + ref[...].astype(F32)
    spread[...] = total
    walk_dev, vectors = out_ref.shape
    lines = vectors // LANES
    for j in range(lines):
        out_ref[:, j * LANES : (j + 1) * LANES] = spread[pl.ds(j, walk_dev, stride=lines), :]


def local(walkers, intersection_inv, new_slot, cholesky):
    devices = lax.axis_size("blk")
    chips = devices // CORES
    walk_dev = walkers.shape[0]
    total = walk_dev * devices
    half = total // 2
    contract = cholesky.shape[0] * cholesky.shape[1]
    vectors = cholesky.shape[2]
    rows = contract // LANES
    inv_rows = intersection_inv.shape[1] // LANES
    inv_blocks = -(-inv_rows // rows)
    blocks = devices + inv_blocks + 1
    share = -(-inv_rows // devices)
    chol = cholesky.reshape(contract, vectors)
    vmem = pl.BlockSpec(memory_space=pltpu.VMEM)
    hbm = pl.BlockSpec(memory_space=pl.ANY)

    def limit(size):
        return pltpu.CompilerParams(vmem_limit_bytes=size)

    place = lax.broadcasted_iota(jnp.int32, (walk_dev, rows * LANES), 1)
    slot = new_slot[:, None]
    number = jnp.where(place < LANES, slot % RADIX, slot // RADIX).astype(BF)
    mine = jnp.concatenate([walkers, intersection_inv, number], axis=1)
    mine = mine.reshape(walk_dev, blocks, rows, LANES)
    swap = [(i, i ^ 1) for i in range(devices)]
    theirs = lax.ppermute(mine, "blk", swap)

    width = 2 * CORES * walk_dev * rows + SLOT_ROWS + CORES * walk_dev * share
    messages = pl.pallas_call(
        pack_kernel,
        in_specs=[vmem, vmem],
        out_specs=[vmem] * chips,
        out_shape=[jax.ShapeDtypeStruct((width, LANES), BF)] * chips,
        scratch_shapes=[pltpu.VMEM((CORES * walk_dev * inv_rows, LANES), F32)],
        compiler_params=limit(8 << 20),
    )(mine, theirs)
    got = exchange(messages, chips)

    step = min(LANES, contract // 4)
    early = contract // 4 // step * step
    pieces = 8
    early_call = pl.pallas_call(
        prefetch_kernel,
        in_specs=[hbm],
        out_specs=vmem,
        out_shape=jax.ShapeDtypeStruct((early, vectors), BF),
        scratch_shapes=[pltpu.SemaphoreType.DMA((pieces,))],
        compiler_params=limit(2 << 20),
        cost_estimate=pl.CostEstimate(
            flops=8_000_000_000, bytes_accessed=early * vectors * 2, transcendentals=0
        ),
    )
    early_chol = early_call(chol)

    greens, back = pl.pallas_call(
        sort_kernel,
        in_specs=[vmem] * chips,
        out_specs=[vmem, vmem],
        out_shape=[
            jax.ShapeDtypeStruct((total, contract), BF),
            jax.ShapeDtypeStruct((devices, walk_dev * (rows + share), LANES), BF),
        ],
        scratch_shapes=[
            pltpu.VMEM((rows * total, LANES), F32),
            pltpu.VMEM((chips, LANES), jnp.int32),
            pltpu.SMEM((chips, LANES), jnp.int32),
            pltpu.SemaphoreType.DMA,
        ],
        compiler_params=limit(8 << 20),
    )(*got)

    ring = min(8, (contract - early) // step)
    send, keep = pl.pallas_call(
        bias_kernel,
        in_specs=[vmem, vmem, hbm],
        out_specs=[vmem, vmem],
        out_shape=[jax.ShapeDtypeStruct((half, vectors), F32)] * 2,
        scratch_shapes=[
            pltpu.VMEM((ring, step, vectors), BF),
            pltpu.SemaphoreType.DMA((ring,)),
        ],
        compiler_params=limit(ring * step * vectors * 2 + half * vectors * 8 + (4 << 20)),
        cost_estimate=pl.CostEstimate(
            flops=20_000_000_000, bytes_accessed=(contract - early) * vectors * 2, transcendentals=0
        ),
    )(greens, early_chol, chol)
    send, keep, back = lax.optimization_barrier((send, keep, back))

    moved = lax.all_to_all(back, "blk", split_axis=0, concat_axis=0, tiled=True)
    moved_walk = (
        moved[:, : walk_dev * rows]
        .reshape(devices, walk_dev, rows, LANES)
        .transpose(1, 0, 2, 3)
        .reshape(walkers.shape)
    )
    moved_inverse = (
        moved[:, walk_dev * rows :]
        .reshape(devices, walk_dev, share * LANES)
        .transpose(1, 0, 2)
        .reshape(walk_dev, devices * share * LANES)[:, : intersection_inv.shape[1]]
    )

    other = lax.ppermute(send, "blk", swap)
    lines = vectors // LANES
    fold_call = pl.pallas_call(
        fold_kernel,
        in_specs=[vmem, vmem],
        out_specs=[vmem] * chips,
        out_shape=[jax.ShapeDtypeStruct((walk_dev * lines, LANES), BF)] * chips,
        scratch_shapes=[pltpu.VMEM((half * lines, LANES), F32)],
        compiler_params=limit(half * vectors * 16 + (2 << 20)),
    )
    shares = fold_call(keep, other)
    shares = exchange(shares, chips)
    bias = pl.pallas_call(
        sum_kernel,
        in_specs=[vmem] * chips,
        out_specs=vmem,
        out_shape=jax.ShapeDtypeStruct((walk_dev, vectors), F32),
        scratch_shapes=[pltpu.VMEM((walk_dev * lines, LANES), F32)],
        compiler_params=limit(chips * walk_dev * vectors * 2 + (2 << 20)),
    )(*shares)
    return moved_walk, moved_inverse, bias


def solution(mesh):
    spec = P(("groups", "blk"), None)
    return jax.shard_map(
        local,
        mesh=mesh,
        in_specs=(spec, spec, P(("groups", "blk")), P(("groups", "blk"), None, None)),
        out_specs=(spec, spec, spec),
        check_vma=False,
    )
```

time: 187 us -> 72 us (0.39)
  waiting for transfers between devices: 89.2 us -> 5.26 us
  blocking collectives: 31.3 us -> 0 us
  matrix products: 30.4 us -> 0 us
  Pallas kernels: 0 us -> 30.4 us
  starting transfers between devices: 11 us -> 30.8 us
  between operations: 15.5 us -> 0.79 us
  local copies, waits for them, and re-layouts: 9.4 us -> 1.68 us
  other arithmetic: 0.01 us -> 2 us
    unnamed x2 -> x0, waiting for transfers between devices: 78.3 us -> none
    dot_general x2 -> x0, matrix products: 30.4 us -> none  [the longest x1 30 us: local(): jnp.dot(green_orbit, chol_flat, preferred_element_type=jnp.float32)]
    pallas_call x0 -> x6, Pallas kernels: none -> 30.4 us  [the longest x1 19.8 us: local(): pl.pallas_call(bias_kernel, in_specs=[vmem, vmem, hbm], out_specs=[vmem,...]
    ppermute x0 -> x16, starting transfers between devices: none -> 24.8 us  [the longest x14 24.2 us: exchange(): got.append(lax.ppermute(messages[k], 'blk', pairs))]
    all_gather x1 -> x0, blocking collectives: 18.9 us -> none  [local(): all_inverse = lax.all_gather(intersection_inv, 'blk', axis=0, tiled=True)]
    unnamed x1 -> x0, blocking collectives: 12.4 us -> none
    all_to_all x2 -> x1, waiting for transfers between devices: 10.8 us -> 0.01 us  [local(): moved = lax.all_to_all(back, 'blk', split_axis=0, concat_axis=0, tiled=True)]
    ppermute x0 -> x16, waiting for transfers between devices: none -> 5.25 us  [the longest x14 4.04 us: exchange(): got.append(lax.ppermute(messages[k], 'blk', pairs))]
  transfers between devices with their start and end apart: 3 -> 17, of which waited for: 2 -> 4; matrix products, arithmetic and copies ran while one was open for 3% -> 2% of each run, Pallas kernels for 0% -> 10%
where the time goes in v2:
time: 72 us; the launch traced here: 70.9 us
  starting transfers between devices  30.8 us (43%)
  Pallas kernels  30.4 us (42%)
  waiting for transfers between devices  5.26 us (7%)
  other arithmetic  2 us (3%)
  local copies, waits for them, and re-layouts  1.68 us (2%)
  between operations  0.79 us (1%)
    ppermute x14, starting transfers between devices, exchange(): got.append(lax.ppermute(messages[k], 'blk', pairs))  24.2 us
    pallas_call x1, Pallas kernels, local(): pl.pallas_call(bias_kernel, in_specs=[vmem, vmem, hbm], out_specs=[vmem,...  19.8 us
    pallas_call x1, Pallas kernels, local(): early_chol = early_call(chol)  7.11 us
    all_to_all x1, starting transfers between devices, local(): moved = lax.all_to_all(back, 'blk', split_axis=0, concat_axis=0, tiled=True)  6.01 us
    ppermute x14, waiting for transfers between devices, exchange(): got.append(lax.ppermute(messages[k], 'blk', pairs))  4.04 us
    pallas_call x1, Pallas kernels, local(): pl.pallas_call(sort_kernel, in_specs=[vmem] * chips, out_specs=[vmem, vme...  1.88 us
  transfers between devices with their start and end apart: 17, of which 4 were waited for; matrix products, arithmetic and copies ran while one was open for 2% of the time, Pallas kernels for 10%

profile of v2, /device:TPU:0, one launch (start us, length us, event | category | flops | bytes accessed | tf_op | source)
XLA Modules:
  0.0 70.9 jit_solution(16941716091345443811)
XLA Ops:
  0.6 0.7 and_select_fusion.1
  1.4 1.2 %maximum_bitcast_fusion = bf16[1,2,576,128]{3,1,2,0:T(2,128)(2,1)S(1)} fusion(bf16[2,4096]{1,0:T(2,128)(2,1)S(1)} %select_convert_fusion, bf16[2,4096]{1,0:T(2,128)(2,1)} %param.5, bf16[2,65536]{1,0:T(2,128)(2,1)} %param.4), kind=kLoop, calls=%fused_computation | loop fusion | flops 884736 | bytes 589824
  3.3 1.2 %collective-permute-done.theirs_ref = bf16[2,18,32,128]{3,2,1,0:T(8,128)(2,1)S(1)} collective-permute-done((bf16[2,18,32,128]{3,2,1,0:T(8,128)(2,1)S(1)}, bf16[2,18,32,128]{3,2,1,0:T(8,128)(2,1)S(1)}, u32[]{:S(2)}, u32[]{:S(2)}) %collective-permute-start) | collective-permute-done | bytes 294944 | tf_op jit(solution)/shard_map/ppermute | solution.py:242
  4.5 0.7 shard_map.67
  5.1 2.9 %collective-permute-start.1 = (bf16[272,128]{1,0:T(8,128)(2,1)S(1)}, bf16[272,128]{1,0:T(8,128)(2,1)S(1)}, u32[]{:S(2)}, u32[]{:S(2)}) collective-permute-start(bf16[272,128]{1,0:T(8,128)(2,1)S(1)} %get-tuple-element.27), channel_id=1, source_target_pairs={{0,2},{1,3},{2,4},{3,5},{4,6},{5,7},{6,8},{7,9},{8,10},{9,11},{10,... | collective-permute-start | bytes 208904 | tf_op jit(solution)/shard_map/ppermute | solution.py:41
  8.1 1.6 %collective-permute-start.2 = (bf16[272,128]{1,0:T(8,128)(2,1)S(1)}, bf16[272,128]{1,0:T(8,128)(2,1)S(1)}, u32[]{:S(2)}, u32[]{:S(2)}) collective-permute-start(bf16[272,128]{1,0:T(8,128)(2,1)S(1)} %get-tuple-element.28), channel_id=1, source_target_pairs={{0,4},{1,5},{2,6},{3,7},{4,8},{5,9},{6,10},{7,11},{8,12},{9,13},{1... | collective-permute-start | bytes 208904 | tf_op jit(solution)/shard_map/ppermute | solution.py:41
  9.6 2.5 %collective-permute-start.3 = (bf16[272,128]{1,0:T(8,128)(2,1)S(1)}, bf16[272,128]{1,0:T(8,128)(2,1)S(1)}, u32[]{:S(2)}, u32[]{:S(2)}) collective-permute-start(bf16[272,128]{1,0:T(8,128)(2,1)S(1)} %get-tuple-element.29), channel_id=1, source_target_pairs={{0,6},{1,7},{2,8},{3,9},{4,10},{5,11},{6,12},{7,13},{8,14},{9,15},... | collective-permute-start | bytes 208904 | tf_op jit(solution)/shard_map/ppermute | solution.py:41
  12.2 1.2 %collective-permute-start.4 = (bf16[272,128]{1,0:T(8,128)(2,1)S(1)}, bf16[272,128]{1,0:T(8,128)(2,1)S(1)}, u32[]{:S(2)}, u32[]{:S(2)}) collective-permute-start(bf16[272,128]{1,0:T(8,128)(2,1)S(1)} %get-tuple-element.30), channel_id=1, source_target_pairs={{0,8},{1,9},{2,10},{3,11},{4,12},{5,13},{6,14},{7,15},{8,0},{9,1},... | collective-permute-start | bytes 208904 | tf_op jit(solution)/shard_map/ppermute | solution.py:41
  13.4 2.6 %collective-permute-start.5 = (bf16[272,128]{1,0:T(8,128)(2,1)S(1)}, bf16[272,128]{1,0:T(8,128)(2,1)S(1)}, u32[]{:S(2)}, u32[]{:S(2)}) collective-permute-start(bf16[272,128]{1,0:T(8,128)(2,1)S(1)} %get-tuple-element.31), channel_id=1, source_target_pairs={{0,10},{1,11},{2,12},{3,13},{4,14},{5,15},{6,0},{7,1},{8,2},{9,3},... | collective-permute-start | bytes 208904 | tf_op jit(solution)/shard_map/ppermute | solution.py:41
  16.1 1.3 %collective-permute-start.6 = (bf16[272,128]{1,0:T(8,128)(2,1)S(1)}, bf16[272,128]{1,0:T(8,128)(2,1)S(1)}, u32[]{:S(2)}, u32[]{:S(2)}) collective-permute-start(bf16[272,128]{1,0:T(8,128)(2,1)S(1)} %get-tuple-element.32), channel_id=1, source_target_pairs={{0,12},{1,13},{2,14},{3,15},{4,0},{5,1},{6,2},{7,3},{8,4},{9,5},{1... | collective-permute-start | bytes 208904 | tf_op jit(solution)/shard_map/ppermute | solution.py:41
  17.4 1.4 %collective-permute-start.7 = (bf16[272,128]{1,0:T(8,128)(2,1)S(1)}, bf16[272,128]{1,0:T(8,128)(2,1)S(1)}, u32[]{:S(2)}, u32[]{:S(2)}) collective-permute-start(bf16[272,128]{1,0:T(8,128)(2,1)S(1)} %get-tuple-element.33), channel_id=1, source_target_pairs={{0,14},{1,15},{2,0},{3,1},{4,2},{5,3},{6,4},{7,5},{8,6},{9,7},{10,... | collective-permute-start | bytes 208904 | tf_op jit(solution)/shard_map/ppermute | solution.py:41
  18.8 7.1 %shard_map.69.early_ref = bf16[1024,10240]{1,0:T(8,128)(2,1)S(1)} custom-call(bf16[4096,10240]{1,0:T(8,128)(2,1)} %bitcast.chol_ref), custom_call_target="tpu_custom_call" | custom-call | flops 8000000000 | bytes 20971520 | tf_op jit(solution)/shard_map/pallas_call | solution.py:269
  26.0 1.9 %shard_map.68 = (bf16[32,4096]{1,0:T(8,128)(2,1)S(1)}, bf16[16,68,128]{2,1,0:T(8,128)(2,1)}) custom-call(bf16[272,128]{1,0:T(8,128)(2,1)S(1)} %get-tuple-element.26.refs_0_, bf16[272,128]{1,0:T(8,128)(2,1)S(1)} %collective-permute-done.1.refs_1_, bf16[272,128]{1,0:T(8,128)(2,1)S(1)} %collective-permute-done.2.refs_2_, ...), custom_call_target="tpu_custom_call" | custom-call | tf_op jit(solution)/shard_map/pallas_call | solution.py:271
  27.9 19.8 %shard_map.70 = (f32[16,10240]{1,0:T(8,128)S(1)}, f32[16,10240]{1,0:T(8,128)S(1)}) custom-call(bf16[32,4096]{1,0:T(8,128)(2,1)S(1)} %get-tuple-element.34.green_ref, bf16[1024,10240]{1,0:T(8,128)(2,1)S(1)} %shard_map.69.early_ref, bf16[4096,10240]{1,0:T(8,128)(2,1)} %bitcast.chol_ref), custom_call_target="tpu_custom_call" | custom-call | flops 20000000000 | bytes 62914560 | tf_op jit(solution)/shard_map/pallas_call | solution.py:289
  47.7 6.0 %all-to-all-start = ((bf16[16,68,128]{2,1,0:T(8,128)(2,1)}), bf16[16,68,128]{2,1,0:T(8,128)(2,1)S(1)}, u32[]{:S(2)}, u32[]{:S(2)}) async-start(bf16[16,68,128]{2,1,0:T(8,128)(2,1)} %get-tuple-element.38), calls=%async_computation | async-start | bytes 589824 | tf_op jit(solution)/shard_map/all_to_all | solution.py:305
  54.0 2.0 %collective-permute-start.9 = (bf16[160,128]{1,0:T(8,128)(2,1)S(1)}, bf16[160,128]{1,0:T(8,128)(2,1)S(1)}, u32[]{:S(2)}, u32[]{:S(2)}) collective-permute-start(bf16[160,128]{1,0:T(8,128)(2,1)S(1)} %get-tuple-element.42), channel_id=1, source_target_pairs={{0,2},{1,3},{2,4},{3,5},{4,6},{5,7},{6,8},{7,9},{8,10},{9,11},{10,... | collective-permute-start | bytes 122888 | tf_op jit(solution)/shard_map/ppermute | solution.py:41
  56.0 1.5 %collective-permute-start.10 = (bf16[160,128]{1,0:T(8,128)(2,1)S(1)}, bf16[160,128]{1,0:T(8,128)(2,1)S(1)}, u32[]{:S(2)}, u32[]{:S(2)}) collective-permute-start(bf16[160,128]{1,0:T(8,128)(2,1)S(1)} %get-tuple-element.43), channel_id=1, source_target_pairs={{0,4},{1,5},{2,6},{3,7},{4,8},{5,9},{6,10},{7,11},{8,12},{9,13},{1... | collective-permute-start | bytes 122888 | tf_op jit(solution)/shard_map/ppermute | solution.py:41
  57.5 2.4 %collective-permute-start.11 = (bf16[160,128]{1,0:T(8,128)(2,1)S(1)}, bf16[160,128]{1,0:T(8,128)(2,1)S(1)}, u32[]{:S(2)}, u32[]{:S(2)}) collective-permute-start(bf16[160,128]{1,0:T(8,128)(2,1)S(1)} %get-tuple-element.44), channel_id=1, source_target_pairs={{0,6},{1,7},{2,8},{3,9},{4,10},{5,11},{6,12},{7,13},{8,14},{9,15},... | collective-permute-start | bytes 122888 | tf_op jit(solution)/shard_map/ppermute | solution.py:41
  59.8 1.5 %collective-permute-start.12 = (bf16[160,128]{1,0:T(8,128)(2,1)S(1)}, bf16[160,128]{1,0:T(8,128)(2,1)S(1)}, u32[]{:S(2)}, u32[]{:S(2)}) collective-permute-start(bf16[160,128]{1,0:T(8,128)(2,1)S(1)} %get-tuple-element.45), channel_id=1, source_target_pairs={{0,8},{1,9},{2,10},{3,11},{4,12},{5,13},{6,14},{7,15},{8,0},{9,1},... | collective-permute-start | bytes 122888 | tf_op jit(solution)/shard_map/ppermute | solution.py:41
  61.3 2.4 %collective-permute-start.13 = (bf16[160,128]{1,0:T(8,128)(2,1)S(1)}, bf16[160,128]{1,0:T(8,128)(2,1)S(1)}, u32[]{:S(2)}, u32[]{:S(2)}) collective-permute-start(bf16[160,128]{1,0:T(8,128)(2,1)S(1)} %get-tuple-element.46), channel_id=1, source_target_pairs={{0,10},{1,11},{2,12},{3,13},{4,14},{5,15},{6,0},{7,1},{8,2},{9,3},... | collective-permute-start | bytes 122888 | tf_op jit(solution)/shard_map/ppermute | solution.py:41
  63.7 2.1 %collective-permute-done.9.refs_1_ = bf16[160,128]{1,0:T(8,128)(2,1)S(1)} collective-permute-done((bf16[160,128]{1,0:T(8,128)(2,1)S(1)}, bf16[160,128]{1,0:T(8,128)(2,1)S(1)}, u32[]{:S(2)}, u32[]{:S(2)}) %collective-permute-start.9) | collective-permute-done | bytes 40992 | tf_op jit(solution)/shard_map/ppermute | solution.py:41
  66.7 1.0 %copy.12 = bf16[1,2,512,128]{3,1,2,0:T(2,128)(2,1)} copy(bf16[1,2,512,128]{3,2,1,0:T(8,128)(2,1)S(1)} %bitcast.18) | data formatting | bytes 524288
  68.3 1.7 %collective-permute-done.11.refs_3_ = bf16[160,128]{1,0:T(8,128)(2,1)S(1)} collective-permute-done((bf16[160,128]{1,0:T(8,128)(2,1)S(1)}, bf16[160,128]{1,0:T(8,128)(2,1)S(1)}, u32[]{:S(2)}, u32[]{:S(2)}) %collective-permute-start.11) | collective-permute-done | bytes 40992 | tf_op jit(solution)/shard_map/ppermute | solution.py:41
  70.2 0.7 %shard_map.72 = f32[2,10240]{1,0:T(2,128)} custom-call(bf16[160,128]{1,0:T(8,128)(2,1)S(1)} %get-tuple-element.41.refs_0_, bf16[160,128]{1,0:T(8,128)(2,1)S(1)} %collective-permute-done.9.refs_1_, bf16[160,128]{1,0:T(8,128)(2,1)S(1)} %collective-permute-done.10.refs_2_, bf16[160,128]{1,0:T(8,128)(2,1)S(1)} %collective-permute-done.11.refs_3_, ...), custom_call_target="tpu_custom_call" | custom-call | tf_op jit(solution)/shard_map/pallas_call | solution.py:331
  (26 shorter events, 2.9 us)
Async XLA Ops:
  2.7 1.8 %collective-permute-start = (bf16[2,18,32,128]{3,2,1,0:T(8,128)(2,1)S(1)}, bf16[2,18,32,128]{3,2,1,0:T(8,128)(2,1)S(1)}, u32[]{:S(2)}, u32[]{:S(2)}) collective-permute-start(bf16[2,18,32,128]{3,2,1,0:T(8,128)(2,1)S(1)} %bitcast.16), channel_id=1, source_target_pairs={{0,1},{1,0},{2,3},{3,2},{4,5},{5,4},{6,7},{7,6},{8,9},{9,8},{10,11... | collective-permute-start | bytes 884744 | tf_op jit(solution)/shard_map/ppermute | solution.py:242
  5.1 10.9 %collective-permute-start.1 = (bf16[272,128]{1,0:T(8,128)(2,1)S(1)}, bf16[272,128]{1,0:T(8,128)(2,1)S(1)}, u32[]{:S(2)}, u32[]{:S(2)}) collective-permute-start(bf16[272,128]{1,0:T(8,128)(2,1)S(1)} %get-tuple-element.27), channel_id=1, source_target_pairs={{0,2},{1,3},{2,4},{3,5},{4,6},{5,7},{6,8},{7,9},{8,10},{9,11},{10,... | collective-permute-start | bytes 208904 | tf_op jit(solution)/shard_map/ppermute | solution.py:41
  8.1 9.3 %collective-permute-start.2 = (bf16[272,128]{1,0:T(8,128)(2,1)S(1)}, bf16[272,128]{1,0:T(8,128)(2,1)S(1)}, u32[]{:S(2)}, u32[]{:S(2)}) collective-permute-start(bf16[272,128]{1,0:T(8,128)(2,1)S(1)} %get-tuple-element.28), channel_id=1, source_target_pairs={{0,4},{1,5},{2,6},{3,7},{4,8},{5,9},{6,10},{7,11},{8,12},{9,13},{1... | collective-permute-start | bytes 208904 | tf_op jit(solution)/shard_map/ppermute | solution.py:41
  9.6 16.3 %collective-permute-start.3 = (bf16[272,128]{1,0:T(8,128)(2,1)S(1)}, bf16[272,128]{1,0:T(8,128)(2,1)S(1)}, u32[]{:S(2)}, u32[]{:S(2)}) collective-permute-start(bf16[272,128]{1,0:T(8,128)(2,1)S(1)} %get-tuple-element.29), channel_id=1, source_target_pairs={{0,6},{1,7},{2,8},{3,9},{4,10},{5,11},{6,12},{7,13},{8,14},{9,15},... | collective-permute-start | bytes 208904 | tf_op jit(solution)/shard_map/ppermute | solution.py:41
  12.2 13.8 %collective-permute-start.4 = (bf16[272,128]{1,0:T(8,128)(2,1)S(1)}, bf16[272,128]{1,0:T(8,128)(2,1)S(1)}, u32[]{:S(2)}, u32[]{:S(2)}) collective-permute-start(bf16[272,128]{1,0:T(8,128)(2,1)S(1)} %get-tuple-element.30), channel_id=1, source_target_pairs={{0,8},{1,9},{2,10},{3,11},{4,12},{5,13},{6,14},{7,15},{8,0},{9,1},... | collective-permute-start | bytes 208904 | tf_op jit(solution)/shard_map/ppermute | solution.py:41
  13.4 12.6 %collective-permute-start.5 = (bf16[272,128]{1,0:T(8,128)(2,1)S(1)}, bf16[272,128]{1,0:T(8,128)(2,1)S(1)}, u32[]{:S(2)}, u32[]{:S(2)}) collective-permute-start(bf16[272,128]{1,0:T(8,128)(2,1)S(1)} %get-tuple-element.31), channel_id=1, source_target_pairs={{0,10},{1,11},{2,12},{3,13},{4,14},{5,15},{6,0},{7,1},{8,2},{9,3},... | collective-permute-start | bytes 208904 | tf_op jit(solution)/shard_map/ppermute | solution.py:41
  16.1 9.9 %collective-permute-start.6 = (bf16[272,128]{1,0:T(8,128)(2,1)S(1)}, bf16[272,128]{1,0:T(8,128)(2,1)S(1)}, u32[]{:S(2)}, u32[]{:S(2)}) collective-permute-start(bf16[272,128]{1,0:T(8,128)(2,1)S(1)} %get-tuple-element.32), channel_id=1, source_target_pairs={{0,12},{1,13},{2,14},{3,15},{4,0},{5,1},{6,2},{7,3},{8,4},{9,5},{1... | collective-permute-start | bytes 208904 | tf_op jit(solution)/shard_map/ppermute | solution.py:41
  17.4 8.6 %collective-permute-start.7 = (bf16[272,128]{1,0:T(8,128)(2,1)S(1)}, bf16[272,128]{1,0:T(8,128)(2,1)S(1)}, u32[]{:S(2)}, u32[]{:S(2)}) collective-permute-start(bf16[272,128]{1,0:T(8,128)(2,1)S(1)} %get-tuple-element.33), channel_id=1, source_target_pairs={{0,14},{1,15},{2,0},{3,1},{4,2},{5,3},{6,4},{7,5},{8,6},{9,7},{10,... | collective-permute-start | bytes 208904 | tf_op jit(solution)/shard_map/ppermute | solution.py:41
  47.7 6.1 %collective-permute-start.8 = (f32[16,10240]{1,0:T(8,128)S(1)}, f32[16,10240]{1,0:T(8,128)S(1)}, u32[]{:S(2)}, u32[]{:S(2)}) collective-permute-start(f32[16,10240]{1,0:T(8,128)S(1)} %get-tuple-element.40), channel_id=1, source_target_pairs={{0,1},{1,0},{2,3},{3,2},{4,5},{5,4},{6,7},{7,6},{8,9},{9,8},{10,11... | collective-permute-start | bytes 1966088 | tf_op jit(solution)/shard_map/ppermute | solution.py:319
  47.7 18.9 %all-to-all-start = ((bf16[16,68,128]{2,1,0:T(8,128)(2,1)}), bf16[16,68,128]{2,1,0:T(8,128)(2,1)S(1)}, u32[]{:S(2)}, u32[]{:S(2)}) async-start(bf16[16,68,128]{2,1,0:T(8,128)(2,1)} %get-tuple-element.38), calls=%async_computation | async-start | bytes 589824 | tf_op jit(solution)/shard_map/all_to_all | solution.py:305
  54.0 11.7 %collective-permute-start.9 = (bf16[160,128]{1,0:T(8,128)(2,1)S(1)}, bf16[160,128]{1,0:T(8,128)(2,1)S(1)}, u32[]{:S(2)}, u32[]{:S(2)}) collective-permute-start(bf16[160,128]{1,0:T(8,128)(2,1)S(1)} %get-tuple-element.42), channel_id=1, source_target_pairs={{0,2},{1,3},{2,4},{3,5},{4,6},{5,7},{6,8},{7,9},{8,10},{9,11},{10,... | collective-permute-start | bytes 122888 | tf_op jit(solution)/shard_map/ppermute | solution.py:41
  56.0 10.0 %collective-permute-start.10 = (bf16[160,128]{1,0:T(8,128)(2,1)S(1)}, bf16[160,128]{1,0:T(8,128)(2,1)S(1)}, u32[]{:S(2)}, u32[]{:S(2)}) collective-permute-start(bf16[160,128]{1,0:T(8,128)(2,1)S(1)} %get-tuple-element.43), channel_id=1, source_target_pairs={{0,4},{1,5},{2,6},{3,7},{4,8},{5,9},{6,10},{7,11},{8,12},{9,13},{1... | collective-permute-start | bytes 122888 | tf_op jit(solution)/shard_map/ppermute | solution.py:41
  57.5 12.5 %collective-permute-start.11 = (bf16[160,128]{1,0:T(8,128)(2,1)S(1)}, bf16[160,128]{1,0:T(8,128)(2,1)S(1)}, u32[]{:S(2)}, u32[]{:S(2)}) collective-permute-start(bf16[160,128]{1,0:T(8,128)(2,1)S(1)} %get-tuple-element.44), channel_id=1, source_target_pairs={{0,6},{1,7},{2,8},{3,9},{4,10},{5,11},{6,12},{7,13},{8,14},{9,15},... | collective-permute-start | bytes 122888 | tf_op jit(solution)/shard_map/ppermute | solution.py:41
  59.8 10.1 %collective-permute-start.12 = (bf16[160,128]{1,0:T(8,128)(2,1)S(1)}, bf16[160,128]{1,0:T(8,128)(2,1)S(1)}, u32[]{:S(2)}, u32[]{:S(2)}) collective-permute-start(bf16[160,128]{1,0:T(8,128)(2,1)S(1)} %get-tuple-element.45), channel_id=1, source_target_pairs={{0,8},{1,9},{2,10},{3,11},{4,12},{5,13},{6,14},{7,15},{8,0},{9,1},... | collective-permute-start | bytes 122888 | tf_op jit(solution)/shard_map/ppermute | solution.py:41
  61.3 8.6 %collective-permute-start.13 = (bf16[160,128]{1,0:T(8,128)(2,1)S(1)}, bf16[160,128]{1,0:T(8,128)(2,1)S(1)}, u32[]{:S(2)}, u32[]{:S(2)}) collective-permute-start(bf16[160,128]{1,0:T(8,128)(2,1)S(1)} %get-tuple-element.46), channel_id=1, source_target_pairs={{0,10},{1,11},{2,12},{3,13},{4,14},{5,15},{6,0},{7,1},{8,2},{9,3},... | collective-permute-start | bytes 122888 | tf_op jit(solution)/shard_map/ppermute | solution.py:41
  65.7 4.5 %collective-permute-start.14 = (bf16[160,128]{1,0:T(8,128)(2,1)S(1)}, bf16[160,128]{1,0:T(8,128)(2,1)S(1)}, u32[]{:S(2)}, u32[]{:S(2)}) collective-permute-start(bf16[160,128]{1,0:T(8,128)(2,1)S(1)} %get-tuple-element.47), channel_id=1, source_target_pairs={{0,12},{1,13},{2,14},{3,15},{4,0},{5,1},{6,2},{7,3},{8,4},{9,5},{1... | collective-permute-start | bytes 122888 | tf_op jit(solution)/shard_map/ppermute | solution.py:41
  66.0 4.2 %collective-permute-start.15 = (bf16[160,128]{1,0:T(8,128)(2,1)S(1)}, bf16[160,128]{1,0:T(8,128)(2,1)S(1)}, u32[]{:S(2)}, u32[]{:S(2)}) collective-permute-start(bf16[160,128]{1,0:T(8,128)(2,1)S(1)} %get-tuple-element.48), channel_id=1, source_target_pairs={{0,14},{1,15},{2,0},{3,1},{4,2},{5,3},{6,4},{7,5},{8,6},{9,7},{10,... | collective-permute-start | bytes 122888 | tf_op jit(solution)/shard_map/ppermute | solution.py:41

commit v3 on v2

v3 whole, which is shorter than its diff:
```python
import jax
import jax.numpy as jnp
from jax import lax
from jax.experimental import pallas as pl
from jax.experimental.pallas import tpu as pltpu
from jax.sharding import PartitionSpec as P


BF = jnp.bfloat16
F32 = jnp.float32
LANES = 128
SLOT_ROWS = 4
RADIX = 256
CORES = 2
DIRECT_CHIPS = 8
EARLY = 6


def paired(chips):
    return chips & (chips - 1) == 0


def apart(chip, k, chips):
    if isinstance(chip, int):
        return chip ^ k if paired(chips) else (chip + k) % chips
    return lax.bitwise_xor(chip, k) if paired(chips) else lax.rem(chip + k, chips)


def away(k, chips):
    return (chips - k) % chips


def my_core():
    return lax.rem(lax.axis_index("blk"), CORES)


def target_chip(k, chips):
    if chips > DIRECT_CHIPS:
        return k
    return apart(lax.div(lax.axis_index("blk"), CORES), away(k, chips), chips)


def source_chip(k, chips):
    if chips > DIRECT_CHIPS:
        return k
    k = away(k, chips)
    return apart(lax.div(lax.axis_index("blk"), CORES), k if paired(chips) else chips - k, chips)


def exchange(messages, chips):
    if chips > DIRECT_CHIPS:
        groups = [[CORES * c + p for c in range(chips)] for p in range(CORES)]
        got = lax.all_to_all(
            jnp.stack(messages),
            "blk",
            split_axis=0,
            concat_axis=0,
            tiled=True,
            axis_index_groups=groups,
        )
        return [got[k] for k in range(chips)]
    got = list(messages)
    for k in range(1, chips):
        pairs = [
            (i, apart(i // CORES, away(k, chips), chips) * CORES + i % CORES) for i in range(chips * CORES)
        ]
        got[k] = lax.ppermute(messages[k], "blk", pairs)
    return got


def fill_parts(slots, walk_ref, inv_ref, inverse, tile, parts):
    chips = len(parts)
    devices, block, _ = walk_ref.shape
    walk_dev = len(slots)
    inv_lines = inv_ref.shape[0]
    inv_rows = inv_lines // walk_dev
    occupied = int(round((LANES * inv_rows) ** 0.5))
    group = LANES // occupied
    share = -(-inv_rows // devices)
    lines = share * walk_dev
    core = my_core()
    targets = [CORES * target_chip(k, chips) + core for k in range(chips)]
    new_row = lax.broadcasted_iota(jnp.int32, (occupied, occupied), 0)
    old_row = lax.broadcasted_iota(jnp.int32, (occupied, occupied), 1)
    order = (
        old_row == lax.rem(new_row, group) * (occupied // group) + lax.div(new_row, group)
    ).astype(BF)
    line = lax.broadcasted_iota(jnp.int32, (chips * block, LANES), 0)
    tile[...] = jnp.zeros_like(tile)
    inverse[...] = inv_ref[...].astype(F32)
    coefficients = jnp.concatenate([walk_ref[t] for t in targets], 0)
    greens = None
    for w in range(walk_dev):
        flat = inverse[pl.ds(w, inv_rows, stride=walk_dev), :].astype(BF)
        split = jnp.concatenate(
            [flat[:, a * occupied : (a + 1) * occupied] for a in range(group)], 0
        )
        inv = jnp.dot(order, split, preferred_element_type=F32).astype(BF)
        zero = jnp.zeros_like(inv)
        both = jnp.concatenate(
            [
                jnp.concatenate([inv if a == b else zero for b in range(group)], 1)
                for a in range(group)
            ],
            0,
        )
        mine = lax.dot_general(
            coefficients, both, (((1,), (1,)), ((), ())), preferred_element_type=F32
        )
        greens = mine if w == 0 else jnp.where(lax.rem(line, walk_dev) == w, mine, greens)
        tile[0:1, w : w + 1] = lax.rem(slots[w], RADIX).astype(F32)
        tile[1:2, w : w + 1] = lax.div(slots[w], RADIX).astype(F32)
    greens = greens.astype(BF)
    for k, put in enumerate(parts):
        piece = slice(k * block, (k + 1) * block)
        put(0, greens[piece])
        put(block, coefficients[piece])
        first = jnp.minimum(targets[k] * share, inv_rows - share) * walk_dev
        put(2 * block, inverse[pl.ds(first, lines), :].astype(BF))
        put(2 * block + lines, tile[...].astype(BF))


def putter(ref, *index, start=0):
    def put(at, value):
        ref[(*index, slice(start + at, start + at + value.shape[0]), slice(None))] = value

    return put


def own_kernel(
    slot_hbm, walk_hbm, inv_hbm, out_ref, slot_ref, walk_ref, inv_ref, inverse, tile, sem
):
    copies = [
        pltpu.make_async_copy(source, target, sem.at[i])
        for i, (source, target) in enumerate(
            ((walk_hbm, walk_ref), (inv_hbm, inv_ref), (slot_hbm, slot_ref))
        )
    ]
    for copy in copies:
        copy.start()
    for copy in copies:
        copy.wait()
    slots = [jnp.full((1, 1), slot_ref[w], jnp.int32) for w in range(slot_ref.shape[0])]
    parts = [putter(out_ref, k) for k in range(out_ref.shape[0])]
    fill_parts(slots, walk_ref, inv_ref, inverse, tile, parts)


def pack_kernel(own_ref, slot_ref, walk_ref, inv_ref, *refs):
    *out_refs, inverse, tile = refs
    size = own_ref.shape[1]
    for k, ref in enumerate(out_refs):
        ref[:size, :] = own_ref[k]
    slots = [slot_ref[0:1, w : w + 1] for w in range(slot_ref.shape[1])]
    parts = [putter(ref, start=size) for ref in out_refs]
    fill_parts(slots, walk_ref, inv_ref, inverse, tile, parts)


def prefetch_kernel(chol_ref, out_ref, sem):
    pieces = sem.shape[0]
    size = out_ref.shape[0] // pieces
    copies = [
        pltpu.make_async_copy(
            chol_ref.at[pl.ds(q * size, size)], out_ref.at[pl.ds(q * size, size)], sem.at[q]
        )
        for q in range(pieces)
    ]
    for copy in copies:
        copy.start()
    for copy in copies:
        copy.wait()


def bias_kernel(*refs):
    *got_refs, early_ref, chol_ref, send_ref, keep_ref, back_send, back_keep = refs[:-9]
    buf, sem, green, text, spread, back, seats, seat_smem, seat_sem = refs[-9:]
    chips = len(got_refs)
    total, contract = green.shape
    early = early_ref.shape[0]
    slots, step, _ = buf.shape
    half = total // 2
    walk_dev = half // chips
    rows = contract // LANES
    block = rows * walk_dev
    back_rows = back_send.shape[1]
    lines = back_rows - block
    size = got_refs[0].shape[0] // CORES
    base = 2 * block + lines
    count = (contract - early) // step

    def copy(i):
        return pltpu.make_async_copy(
            chol_ref.at[pl.ds(early + i * step, step)], buf.at[i % slots], sem.at[i % slots]
        )

    for i in range(min(slots, count)):
        copy(i).start()

    for m in range(chips):
        for n in range(CORES):
            at = n * size + base
            low = got_refs[m][at : at + 1, :].astype(F32)
            high = got_refs[m][at + 1 : at + 2, :].astype(F32)
            at = m * CORES + n
            seats[at : at + 1, :] = (low + RADIX * high).astype(jnp.int32)
    seat_copy = pltpu.make_async_copy(seats, seat_smem, seat_sem)
    seat_copy.start()
    seat_copy.wait()
    core = my_core()
    for m in range(chips):
        text[m] = got_refs[m][...].astype(F32)
        for n in range(CORES):
            for w in range(walk_dev):
                at = n * size + w
                owner = lax.div(seat_smem[m * CORES + n, w], walk_dev)
                side = jnp.where(lax.rem(owner, CORES) == core, 1, 0)
                chip = lax.div(owner, CORES)
                seat = (side * walk_dev + w) * chips + chip
                spread[pl.ds(seat, rows, stride=total), :] = text[
                    m, pl.ds(at, rows, stride=walk_dev), :
                ]
                first = (side * chips + chip) * back_rows + w
                back[pl.ds(first, rows, stride=walk_dev), :] = text[
                    m, pl.ds(at + block, rows, stride=walk_dev), :
                ]
                for q in range(0, lines, walk_dev):
                    line = at + 2 * block + q
                    back[pl.ds(first + block + q, 1), :] = text[m, line : line + 1, :]
    for r in range(rows):
        green[:, r * LANES : (r + 1) * LANES] = spread[r * total : (r + 1) * total, :].astype(BF)
    for c in range(chips):
        back_send[c] = back[c * back_rows : (c + 1) * back_rows, :].astype(BF)
        at = (chips + c) * back_rows
        back_keep[c] = back[at : at + back_rows, :].astype(BF)

    part = jnp.dot(green[:, :early], early_ref[...], preferred_element_type=F32)
    send_ref[...] = part[:half]
    keep_ref[...] = part[half:]
    for i in range(count):
        copy(i).wait()
        part = jnp.dot(
            green[:, early + i * step : early + (i + 1) * step],
            buf[i % slots],
            preferred_element_type=F32,
        )
        send_ref[...] += part[:half]
        keep_ref[...] += part[half:]
        if i + slots < count:
            copy(i + slots).start()


def fold_kernel(keep_ref, got_ref, back_keep, back_got, *refs):
    *out_refs, spread = refs
    chips = len(out_refs)
    half, vectors = keep_ref.shape
    walk_dev = half // chips
    size = vectors // LANES * walk_dev
    back_rows = back_keep.shape[1]
    for j in range(vectors // LANES):
        at = slice(j * LANES, (j + 1) * LANES)
        both = keep_ref[:, at] + got_ref[:, at]
        for w in range(walk_dev):
            spread[pl.ds(j * walk_dev + w, chips, stride=size), :] = both[
                w * chips : (w + 1) * chips
            ]
    for k in range(chips):
        chip = target_chip(k, chips)
        first = chip * size
        if not isinstance(first, int):
            first = pl.multiple_of(first, 8)
        out_refs[k][:size, :] = spread[pl.ds(first, size), :].astype(BF)
        out_refs[k][size : size + back_rows, :] = back_keep[chip]
        out_refs[k][size + back_rows :, :] = back_got[chip]


def last_kernel(*refs):
    *got_refs, bias_ref, walk_ref, inv_ref, inverse = refs
    chips = len(got_refs)
    devices, block, _ = walk_ref.shape
    size = bias_ref.shape[0]
    lines = inverse.shape[0] // devices
    total = got_refs[0][:size, :].astype(F32)
    for ref in got_refs[1:]:
        total = total + ref[:size, :].astype(F32)
    bias_ref[...] = total
    core = my_core()
    for k in range(chips):
        chip = CORES * source_chip(k, chips)
        for n, device in enumerate((chip + core, chip + 1 - core)):
            at = size + n * (block + lines)
            walk_ref[device] = got_refs[k][at : at + block, :]
            inverse[pl.ds(device * lines, lines), :] = got_refs[k][
                at + block : at + block + lines, :
            ].astype(F32)
    inv_ref[...] = inverse[: inv_ref.shape[0], :].astype(BF)


def lines_of(x):
    count, size = x.shape
    x = x.reshape(count, size // LANES, LANES).transpose(1, 0, 2)
    return x.reshape(count * size // LANES, LANES)


def walkers_of(x, count):
    return x.reshape(-1, count, LANES).transpose(1, 0, 2).reshape(count, -1)


def local(walkers, intersection_inv, new_slot, cholesky):
    devices = lax.axis_size("blk")
    chips = devices // CORES
    walk_dev = walkers.shape[0]
    total = walk_dev * devices
    half = total // 2
    contract = cholesky.shape[0] * cholesky.shape[1]
    vectors = cholesky.shape[2]
    rows = contract // LANES
    block = rows * walk_dev
    inv_rows = intersection_inv.shape[1] // LANES
    lines = -(-inv_rows // devices) * walk_dev
    chol = cholesky.reshape(contract, vectors)
    vmem = pl.BlockSpec(memory_space=pltpu.VMEM)
    far = pl.BlockSpec(memory_space=pltpu.HBM)
    hbm = pl.BlockSpec(memory_space=pl.ANY)

    def limit(size):
        return pltpu.CompilerParams(vmem_limit_bytes=size)

    def out(*shape, dtype=BF):
        return jax.ShapeDtypeStruct(shape, dtype)

    swap = [(i, i ^ 1) for i in range(devices)]

    part = 2 * block + lines + SLOT_ROWS
    width = CORES * part
    walk = lines_of(walkers).reshape(devices, block, LANES)
    inverse = lines_of(intersection_inv)
    own_call = pl.pallas_call(
        own_kernel,
        in_specs=[far, far, far],
        out_specs=vmem,
        out_shape=pltpu.VMEM((chips, part, LANES), BF),
        scratch_shapes=[
            pltpu.SMEM(new_slot.shape, jnp.int32),
            pltpu.VMEM(walk.shape, BF),
            pltpu.VMEM(inverse.shape, BF),
            pltpu.VMEM(inverse.shape, F32),
            pltpu.VMEM((SLOT_ROWS, LANES), F32),
            pltpu.SemaphoreType.DMA((3,)),
        ],
        compiler_params=limit(8 << 20),
        cost_estimate=pl.CostEstimate(flops=500_000_000, bytes_accessed=0, transcendentals=0),
    )
    their_walk = lax.ppermute(walk, "blk", swap)
    their_inverse = lax.ppermute(inverse, "blk", swap)
    their_slot = lax.ppermute(new_slot.reshape(1, walk_dev), "blk", swap)
    own = own_call(
        *(
            pltpu.with_memory_space_constraint(x, pltpu.HBM)
            for x in (new_slot, walk, inverse)
        )
    )
    messages = pl.pallas_call(
        pack_kernel,
        in_specs=[vmem] * 4,
        out_specs=[vmem] * chips,
        out_shape=[out(width, LANES)] * chips,
        scratch_shapes=[pltpu.VMEM(inverse.shape, F32), pltpu.VMEM((SLOT_ROWS, LANES), F32)],
        compiler_params=limit(8 << 20),
    )(own, their_slot, their_walk, their_inverse)
    got = exchange(messages, chips)

    step = min(LANES, contract // 4)
    early = max(step, contract * EARLY // 32 // step * step)
    pieces = 8
    early_call = pl.pallas_call(
        prefetch_kernel,
        in_specs=[hbm],
        out_specs=vmem,
        out_shape=out(early, vectors),
        scratch_shapes=[pltpu.SemaphoreType.DMA((pieces,))],
        compiler_params=limit(2 << 20),
        cost_estimate=pl.CostEstimate(
            flops=8_000_000_000, bytes_accessed=early * vectors * 2, transcendentals=0
        ),
    )
    early_chol = early_call(chol)

    ring = min(8, (contract - early) // step)
    back_rows = block + lines
    send, keep, back_send, back_keep = pl.pallas_call(
        bias_kernel,
        in_specs=[vmem] * (chips + 1) + [hbm],
        out_specs=[vmem] * 4,
        out_shape=[out(half, vectors, dtype=F32)] * 2 + [out(chips, back_rows, LANES)] * 2,
        scratch_shapes=[
            pltpu.VMEM((ring, step, vectors), BF),
            pltpu.SemaphoreType.DMA((ring,)),
            pltpu.VMEM((total, contract), BF),
            pltpu.VMEM((chips, width, LANES), F32),
            pltpu.VMEM((rows * total, LANES), F32),
            pltpu.VMEM((2 * chips * back_rows, LANES), F32),
            pltpu.VMEM((chips * CORES, LANES), jnp.int32),
            pltpu.SMEM((chips * CORES, LANES), jnp.int32),
            pltpu.SemaphoreType.DMA,
        ],
        compiler_params=limit(ring * step * vectors * 2 + half * vectors * 8 + (8 << 20)),
        cost_estimate=pl.CostEstimate(
            flops=20_000_000_000, bytes_accessed=(contract - early) * vectors * 2, transcendentals=0
        ),
    )(*got, early_chol, chol)

    other = lax.ppermute(send, "blk", swap)
    back_other = lax.ppermute(back_send, "blk", swap)
    size = vectors // LANES * walk_dev
    shares = pl.pallas_call(
        fold_kernel,
        in_specs=[vmem] * 4,
        out_specs=[vmem] * chips,
        out_shape=[out(size + CORES * back_rows, LANES)] * chips,
        scratch_shapes=[pltpu.VMEM((chips * size, LANES), F32)],
        compiler_params=limit(half * vectors * 16 + (4 << 20)),
    )(keep, other, back_keep, back_other)
    shares = exchange(shares, chips)
    bias, moved_walk, moved_inverse = pl.pallas_call(
        last_kernel,
        in_specs=[vmem] * chips,
        out_specs=[vmem] * 3,
        out_shape=[
            out(size, LANES, dtype=F32),
            out(devices, block, LANES),
            out(inv_rows * walk_dev, LANES),
        ],
        scratch_shapes=[pltpu.VMEM((devices * lines, LANES), F32)],
        compiler_params=limit(chips * walk_dev * vectors * 4 + (4 << 20)),
    )(*shares)
    return (
        walkers_of(moved_walk.reshape(devices * block, LANES), walk_dev),
        walkers_of(moved_inverse, walk_dev),
        walkers_of(bias, walk_dev),
    )


def solution(mesh):
    spec = P(("groups", "blk"), None)
    return jax.shard_map(
        local,
        mesh=mesh,
        in_specs=(spec, spec, P(("groups", "blk")), P(("groups", "blk"), None, None)),
        out_specs=(spec, spec, spec),
        check_vma=False,
    )
```

time: 72 us -> 67.4 us (0.936); the launches traced: 70.9 us -> 67.3 us
  other arithmetic: 2 us -> 0 us
  local copies, waits for them, and re-layouts: 1.68 us -> 0 us
  waiting for transfers between devices: 5.26 us -> 6.75 us
  starting transfers between devices: 30.8 us -> 29.7 us
    all_to_all x1 -> x0, starting transfers between devices: 6.01 us -> none  [local(): moved = lax.all_to_all(back, 'blk', split_axis=0, concat_axis=0, tiled=True)]
    ppermute x15 -> x18, starting transfers between devices: 24.7 us -> 29.6 us  [the longest x14 28.1 us: exchange(): got[k] = lax.ppermute(messages[k], 'blk', pairs)]
    pallas_call x1, Pallas kernels: 7.11 us -> 5.61 us  [local(): early_chol = early_call(chol)]
    ppermute x15 -> x18, waiting for transfers between devices: 5.25 us -> 6.75 us  [the longest x14 4.94 us: exchange(): got[k] = lax.ppermute(messages[k], 'blk', pairs)]
    unnamed x1 -> x0, other arithmetic: 1.24 us -> none
    pallas_call x5, Pallas kernels: 23.3 us -> 24.4 us  [the longest x1 21.3 us: local(): pl.pallas_call(bias_kernel, in_specs=[vmem] * (chips + 1) + [hbm], out_sp...]
    unnamed x2 -> x0, local copies, waits for them, and re-layouts: 1.01 us -> none
  transfers between devices with their start and end apart: 17 -> 19, of which waited for: 4 -> 5; matrix products, arithmetic and copies ran while one was open for 2% -> 0% of each run, Pallas kernels for 10% -> 11%
where the time goes in v3:
time: 67.4 us; the launch traced here: 67.3 us
  Pallas kernels  30.1 us (45%)
  starting transfers between devices  29.7 us (44%)
  waiting for transfers between devices  6.75 us (10%)
  between operations  0.76 us (1%)
    ppermute x14, starting transfers between devices, exchange(): got[k] = lax.ppermute(messages[k], 'blk', pairs)  28.1 us
    pallas_call x1, Pallas kernels, local(): pl.pallas_call(bias_kernel, in_specs=[vmem] * (chips + 1) + [hbm], out_sp...  21.3 us
    pallas_call x1, Pallas kernels, local(): early_chol = early_call(chol)  5.61 us
    ppermute x14, waiting for transfers between devices, exchange(): got[k] = lax.ppermute(messages[k], 'blk', pairs)  4.94 us
    ppermute x1, waiting for transfers between devices, local(): back_other = lax.ppermute(back_send, 'blk', swap)  1.8 us
    pallas_call x1, Pallas kernels, local(): own_call(*(pltpu.with_memory_space_constraint(x, pltpu.HBM) for x in (new...  1.46 us
  transfers between devices with their start and end apart: 19, of which 5 were waited for; matrix products, arithmetic and copies ran while one was open for 0% of the time, Pallas kernels for 11%

profile of v3, /device:TPU:0, one launch (start us, length us, event | category | flops | bytes accessed | tf_op | source)
XLA Modules:
  0.0 67.3 jit_solution(17401304201355512231)
XLA Ops:
  0.6 0.6 collective-permute-start.1
  1.7 1.5 %shard_map.67.own_ref = bf16[8,136,128]{2,1,0:T(8,128)(2,1)S(1)} custom-call(s32[2]{0:T(128)} %slot_hbm.1, bf16[16,64,128]{2,1,0:T(8,128)(2,1)} %bitcast.28, bf16[64,128]{1,0:T(8,128)(2,1)} %bitcast.32), custom_call_target="tpu_custom_call" | custom-call | flops 500000000 | tf_op jit(solution)/shard_map/pallas_call | solution.py:355
  3.2 0.5 shard_map.68
  3.7 5.7 %collective-permute-start.3 = (bf16[272,128]{1,0:T(8,128)(2,1)S(1)}, bf16[272,128]{1,0:T(8,128)(2,1)S(1)}, u32[]{:S(2)}, u32[]{:S(2)}) collective-permute-start(bf16[272,128]{1,0:T(8,128)(2,1)S(1)} %get-tuple-element.27), channel_id=1, source_target_pairs={{0,14},{1,15},{2,12},{3,13},{4,10},{5,11},{6,8},{7,9},{8,6},{9,7},... | collective-permute-start | bytes 208904 | tf_op jit(solution)/shard_map/ppermute | solution.py:67
  9.6 0.7 %collective-permute-start.5 = (bf16[272,128]{1,0:T(8,128)(2,1)S(1)}, bf16[272,128]{1,0:T(8,128)(2,1)S(1)}, u32[]{:S(2)}, u32[]{:S(2)}) collective-permute-start(bf16[272,128]{1,0:T(8,128)(2,1)S(1)} %get-tuple-element.29), channel_id=1, source_target_pairs={{0,10},{1,11},{2,8},{3,9},{4,14},{5,15},{6,12},{7,13},{8,2},{9,3},... | collective-permute-start | bytes 208904 | tf_op jit(solution)/shard_map/ppermute | solution.py:67
  10.3 2.0 %collective-permute-start.6 = (bf16[272,128]{1,0:T(8,128)(2,1)S(1)}, bf16[272,128]{1,0:T(8,128)(2,1)S(1)}, u32[]{:S(2)}, u32[]{:S(2)}) collective-permute-start(bf16[272,128]{1,0:T(8,128)(2,1)S(1)} %get-tuple-element.30), channel_id=1, source_target_pairs={{0,8},{1,9},{2,10},{3,11},{4,12},{5,13},{6,14},{7,15},{8,0},{9,1},... | collective-permute-start | bytes 208904 | tf_op jit(solution)/shard_map/ppermute | solution.py:67
  12.4 2.3 %collective-permute-start.7 = (bf16[272,128]{1,0:T(8,128)(2,1)S(1)}, bf16[272,128]{1,0:T(8,128)(2,1)S(1)}, u32[]{:S(2)}, u32[]{:S(2)}) collective-permute-start(bf16[272,128]{1,0:T(8,128)(2,1)S(1)} %get-tuple-element.31), channel_id=1, source_target_pairs={{0,6},{1,7},{2,4},{3,5},{4,2},{5,3},{6,0},{7,1},{8,14},{9,15},{10,... | collective-permute-start | bytes 208904 | tf_op jit(solution)/shard_map/ppermute | solution.py:67
  14.7 0.8 %collective-permute-start.8 = (bf16[272,128]{1,0:T(8,128)(2,1)S(1)}, bf16[272,128]{1,0:T(8,128)(2,1)S(1)}, u32[]{:S(2)}, u32[]{:S(2)}) collective-permute-start(bf16[272,128]{1,0:T(8,128)(2,1)S(1)} %get-tuple-element.32), channel_id=1, source_target_pairs={{0,4},{1,5},{2,6},{3,7},{4,0},{5,1},{6,2},{7,3},{8,12},{9,13},{10,... | collective-permute-start | bytes 208904 | tf_op jit(solution)/shard_map/ppermute | solution.py:67
  15.5 0.9 %collective-permute-done.4.refs_2_ = bf16[272,128]{1,0:T(8,128)(2,1)S(1)} collective-permute-done((bf16[272,128]{1,0:T(8,128)(2,1)S(1)}, bf16[272,128]{1,0:T(8,128)(2,1)S(1)}, u32[]{:S(2)}, u32[]{:S(2)}) %collective-permute-start.4) | collective-permute-done | bytes 69664 | tf_op jit(solution)/shard_map/ppermute | solution.py:67
  16.4 0.5 collective-permute-start.9
  16.9 5.6 %shard_map.69.refs_8_ = bf16[768,10240]{1,0:T(8,128)(2,1)S(1)} custom-call(bf16[4096,10240]{1,0:T(8,128)(2,1)} %bitcast.11.chol_ref.refs_9_), custom_call_target="tpu_custom_call" | custom-call | flops 8000000000 | bytes 15728640 | tf_op jit(solution)/shard_map/pallas_call | solution.py:385
  22.5 21.3 %shard_map.70 = (f32[16,10240]{1,0:T(8,128)S(1)}, f32[16,10240]{1,0:T(8,128)S(1)}, bf16[8,68,128]{2,1,0:T(8,128)(2,1)S(1)}, bf16[8,68,128]{2,1,0:T(8,128)(2,1)S(1)}) custom-call(bf16[272,128]{1,0:T(8,128)(2,1)S(1)} %get-tuple-element.26.refs_0_, bf16[272,128]{1,0:T(8,128)(2,1)S(1)} %collective-permute-done.3.refs_1_, ...), custom_call_target="tpu_custom_call" | custom-call | flops 20000000000 | bytes 68157440 | tf_op jit(solution)/shard_map/pallas_call | solution.py:389
  43.9 0.5 collective-permute-start.11
  44.4 1.8 %collective-permute-done.11.back_got = bf16[8,68,128]{2,1,0:T(8,128)(2,1)S(1)} collective-permute-done((bf16[8,68,128]{2,1,0:T(8,128)(2,1)S(1)}, bf16[8,68,128]{2,1,0:T(8,128)(2,1)S(1)}, u32[]{:S(2)}, u32[]{:S(2)}) %collective-permute-start.11) | collective-permute-done | bytes 139296 | tf_op jit(solution)/shard_map/ppermute | solution.py:412
  46.7 5.0 %collective-permute-start.12 = (bf16[296,128]{1,0:T(8,128)(2,1)S(1)}, bf16[296,128]{1,0:T(8,128)(2,1)S(1)}, u32[]{:S(2)}, u32[]{:S(2)}) collective-permute-start(bf16[296,128]{1,0:T(8,128)(2,1)S(1)} %get-tuple-element.39), channel_id=1, source_target_pairs={{0,14},{1,15},{2,12},{3,13},{4,10},{5,11},{6,8},{7,9},{8,6},{9,7},... | collective-permute-start | bytes 227336 | tf_op jit(solution)/shard_map/ppermute | solution.py:67
  51.8 2.4 %collective-permute-start.14 = (bf16[296,128]{1,0:T(8,128)(2,1)S(1)}, bf16[296,128]{1,0:T(8,128)(2,1)S(1)}, u32[]{:S(2)}, u32[]{:S(2)}) collective-permute-start(bf16[296,128]{1,0:T(8,128)(2,1)S(1)} %get-tuple-element.41), channel_id=1, source_target_pairs={{0,10},{1,11},{2,8},{3,9},{4,14},{5,15},{6,12},{7,13},{8,2},{9,3},... | collective-permute-start | bytes 227336 | tf_op jit(solution)/shard_map/ppermute | solution.py:67
  54.2 1.4 %collective-permute-start.15 = (bf16[296,128]{1,0:T(8,128)(2,1)S(1)}, bf16[296,128]{1,0:T(8,128)(2,1)S(1)}, u32[]{:S(2)}, u32[]{:S(2)}) collective-permute-start(bf16[296,128]{1,0:T(8,128)(2,1)S(1)} %get-tuple-element.42), channel_id=1, source_target_pairs={{0,8},{1,9},{2,10},{3,11},{4,12},{5,13},{6,14},{7,15},{8,0},{9,1},... | collective-permute-start | bytes 227336 | tf_op jit(solution)/shard_map/ppermute | solution.py:67
  55.5 1.5 %collective-permute-start.16 = (bf16[296,128]{1,0:T(8,128)(2,1)S(1)}, bf16[296,128]{1,0:T(8,128)(2,1)S(1)}, u32[]{:S(2)}, u32[]{:S(2)}) collective-permute-start(bf16[296,128]{1,0:T(8,128)(2,1)S(1)} %get-tuple-element.43), channel_id=1, source_target_pairs={{0,6},{1,7},{2,4},{3,5},{4,2},{5,3},{6,0},{7,1},{8,14},{9,15},{10,... | collective-permute-start | bytes 227336 | tf_op jit(solution)/shard_map/ppermute | solution.py:67
  57.0 4.5 %collective-permute-start.17 = (bf16[296,128]{1,0:T(8,128)(2,1)S(1)}, bf16[296,128]{1,0:T(8,128)(2,1)S(1)}, u32[]{:S(2)}, u32[]{:S(2)}) collective-permute-start(bf16[296,128]{1,0:T(8,128)(2,1)S(1)} %get-tuple-element.44), channel_id=1, source_target_pairs={{0,4},{1,5},{2,6},{3,7},{4,0},{5,1},{6,2},{7,3},{8,12},{9,13},{10,... | collective-permute-start | bytes 227336 | tf_op jit(solution)/shard_map/ppermute | solution.py:67
  61.6 0.9 %collective-permute-start.18 = (bf16[296,128]{1,0:T(8,128)(2,1)S(1)}, bf16[296,128]{1,0:T(8,128)(2,1)S(1)}, u32[]{:S(2)}, u32[]{:S(2)}) collective-permute-start(bf16[296,128]{1,0:T(8,128)(2,1)S(1)} %get-tuple-element.45), channel_id=1, source_target_pairs={{0,2},{1,3},{2,0},{3,1},{4,6},{5,7},{6,4},{7,5},{8,10},{9,11},{10,... | collective-permute-start | bytes 227336 | tf_op jit(solution)/shard_map/ppermute | solution.py:67
  62.5 1.7 %collective-permute-done.14.refs_3_ = bf16[296,128]{1,0:T(8,128)(2,1)S(1)} collective-permute-done((bf16[296,128]{1,0:T(8,128)(2,1)S(1)}, bf16[296,128]{1,0:T(8,128)(2,1)S(1)}, u32[]{:S(2)}, u32[]{:S(2)}) %collective-permute-start.14) | collective-permute-done | bytes 75808 | tf_op jit(solution)/shard_map/ppermute | solution.py:67
  64.2 1.6 %collective-permute-done.15.refs_4_ = bf16[296,128]{1,0:T(8,128)(2,1)S(1)} collective-permute-done((bf16[296,128]{1,0:T(8,128)(2,1)S(1)}, bf16[296,128]{1,0:T(8,128)(2,1)S(1)}, u32[]{:S(2)}, u32[]{:S(2)}) %collective-permute-start.15) | collective-permute-done | bytes 75808 | tf_op jit(solution)/shard_map/ppermute | solution.py:67
  65.8 0.7 %collective-permute-done.17.refs_6_ = bf16[296,128]{1,0:T(8,128)(2,1)S(1)} collective-permute-done((bf16[296,128]{1,0:T(8,128)(2,1)S(1)}, bf16[296,128]{1,0:T(8,128)(2,1)S(1)}, u32[]{:S(2)}, u32[]{:S(2)}) %collective-permute-start.17) | collective-permute-done | bytes 75808 | tf_op jit(solution)/shard_map/ppermute | solution.py:67
  66.5 0.8 %shard_map.72 = (f32[160,128]{1,0:T(8,128)}, bf16[16,64,128]{2,1,0:T(8,128)(2,1)}, bf16[64,128]{1,0:T(8,128)(2,1)}) custom-call(bf16[296,128]{1,0:T(8,128)(2,1)S(1)} %get-tuple-element.38.refs_0_, bf16[296,128]{1,0:T(8,128)(2,1)S(1)} %collective-permute-done.12.refs_1_, bf16[296,128]{1,0:T(8,128)(2,1)S(1)} %collective-permute-done.13.refs_2_, ...), custom_call_target="tpu_custom_call" | custom-call | tf_op jit(solution)/shard_map/pallas_call | solution.py:423
  (20 shorter events, 1.4 us)
Async XLA Ops:
  0.6 2.6 %collective-permute-start.1 = (bf16[16,64,128]{2,1,0:T(8,128)(2,1)}, bf16[16,64,128]{2,1,0:T(8,128)(2,1)S(1)}, u32[]{:S(2)}, u32[]{:S(2)}) collective-permute-start(bf16[16,64,128]{2,1,0:T(8,128)(2,1)} %bitcast.27), channel_id=1, source_target_pairs={{0,1},{1,0},{2,3},{3,2},{4,5},{5,4},{6,7},{7,6},{8,9},{9,8},{10,11... | collective-permute-start | bytes 786440 | tf_op jit(solution)/shard_map/ppermute | solution.py:352
  1.2 2.0 %collective-permute-start = (s32[1,2]{1,0:T(1,128)}, s32[1,2]{1,0:T(1,128)S(1)}, u32[]{:S(2)}, u32[]{:S(2)}) collective-permute-start(s32[1,2]{1,0:T(1,128)} %bitcast.34), channel_id=1, source_target_pairs={{0,1},{1,0},{2,3},{3,2},{4,5},{5,4},{6,7},{7,6},{8,9},{9,8},{10,11... | collective-permute-start | bytes 32 | tf_op jit(solution)/shard_map/ppermute | solution.py:354
  1.3 1.9 %collective-permute-start.2 = (bf16[64,128]{1,0:T(8,128)(2,1)}, bf16[64,128]{1,0:T(8,128)(2,1)S(1)}, u32[]{:S(2)}, u32[]{:S(2)}) collective-permute-start(bf16[64,128]{1,0:T(8,128)(2,1)} %bitcast.31), channel_id=1, source_target_pairs={{0,1},{1,0},{2,3},{3,2},{4,5},{5,4},{6,7},{7,6},{8,9},{9,8},{10,11... | collective-permute-start | bytes 49160 | tf_op jit(solution)/shard_map/ppermute | solution.py:353
  3.7 11.0 %collective-permute-start.3 = (bf16[272,128]{1,0:T(8,128)(2,1)S(1)}, bf16[272,128]{1,0:T(8,128)(2,1)S(1)}, u32[]{:S(2)}, u32[]{:S(2)}) collective-permute-start(bf16[272,128]{1,0:T(8,128)(2,1)S(1)} %get-tuple-element.27), channel_id=1, source_target_pairs={{0,14},{1,15},{2,12},{3,13},{4,10},{5,11},{6,8},{7,9},{8,6},{9,7},... | collective-permute-start | bytes 208904 | tf_op jit(solution)/shard_map/ppermute | solution.py:67
  9.4 7.0 %collective-permute-start.4 = (bf16[272,128]{1,0:T(8,128)(2,1)S(1)}, bf16[272,128]{1,0:T(8,128)(2,1)S(1)}, u32[]{:S(2)}, u32[]{:S(2)}) collective-permute-start(bf16[272,128]{1,0:T(8,128)(2,1)S(1)} %get-tuple-element.28), channel_id=1, source_target_pairs={{0,12},{1,13},{2,14},{3,15},{4,8},{5,9},{6,10},{7,11},{8,4},{9,5},... | collective-permute-start | bytes 208904 | tf_op jit(solution)/shard_map/ppermute | solution.py:67
  9.6 12.9 %collective-permute-start.5 = (bf16[272,128]{1,0:T(8,128)(2,1)S(1)}, bf16[272,128]{1,0:T(8,128)(2,1)S(1)}, u32[]{:S(2)}, u32[]{:S(2)}) collective-permute-start(bf16[272,128]{1,0:T(8,128)(2,1)S(1)} %get-tuple-element.29), channel_id=1, source_target_pairs={{0,10},{1,11},{2,8},{3,9},{4,14},{5,15},{6,12},{7,13},{8,2},{9,3},... | collective-permute-start | bytes 208904 | tf_op jit(solution)/shard_map/ppermute | solution.py:67
  10.3 12.2 %collective-permute-start.6 = (bf16[272,128]{1,0:T(8,128)(2,1)S(1)}, bf16[272,128]{1,0:T(8,128)(2,1)S(1)}, u32[]{:S(2)}, u32[]{:S(2)}) collective-permute-start(bf16[272,128]{1,0:T(8,128)(2,1)S(1)} %get-tuple-element.30), channel_id=1, source_target_pairs={{0,8},{1,9},{2,10},{3,11},{4,12},{5,13},{6,14},{7,15},{8,0},{9,1},... | collective-permute-start | bytes 208904 | tf_op jit(solution)/shard_map/ppermute | solution.py:67
  12.4 10.1 %collective-permute-start.7 = (bf16[272,128]{1,0:T(8,128)(2,1)S(1)}, bf16[272,128]{1,0:T(8,128)(2,1)S(1)}, u32[]{:S(2)}, u32[]{:S(2)}) collective-permute-start(bf16[272,128]{1,0:T(8,128)(2,1)S(1)} %get-tuple-element.31), channel_id=1, source_target_pairs={{0,6},{1,7},{2,4},{3,5},{4,2},{5,3},{6,0},{7,1},{8,14},{9,15},{10,... | collective-permute-start | bytes 208904 | tf_op jit(solution)/shard_map/ppermute | solution.py:67
  14.7 7.8 %collective-permute-start.8 = (bf16[272,128]{1,0:T(8,128)(2,1)S(1)}, bf16[272,128]{1,0:T(8,128)(2,1)S(1)}, u32[]{:S(2)}, u32[]{:S(2)}) collective-permute-start(bf16[272,128]{1,0:T(8,128)(2,1)S(1)} %get-tuple-element.32), channel_id=1, source_target_pairs={{0,4},{1,5},{2,6},{3,7},{4,0},{5,1},{6,2},{7,3},{8,12},{9,13},{10,... | collective-permute-start | bytes 208904 | tf_op jit(solution)/shard_map/ppermute | solution.py:67
  16.4 6.2 %collective-permute-start.9 = (bf16[272,128]{1,0:T(8,128)(2,1)S(1)}, bf16[272,128]{1,0:T(8,128)(2,1)S(1)}, u32[]{:S(2)}, u32[]{:S(2)}) collective-permute-start(bf16[272,128]{1,0:T(8,128)(2,1)S(1)} %get-tuple-element.33), channel_id=1, source_target_pairs={{0,2},{1,3},{2,0},{3,1},{4,6},{5,7},{6,4},{7,5},{8,10},{9,11},{10,... | collective-permute-start | bytes 208904 | tf_op jit(solution)/shard_map/ppermute | solution.py:67
  43.8 2.4 %collective-permute-start.10 = (f32[16,10240]{1,0:T(8,128)S(1)}, f32[16,10240]{1,0:T(8,128)S(1)}, u32[]{:S(2)}, u32[]{:S(2)}) collective-permute-start(f32[16,10240]{1,0:T(8,128)S(1)} %get-tuple-element.35), channel_id=1, source_target_pairs={{0,1},{1,0},{2,3},{3,2},{4,5},{5,4},{6,7},{7,6},{8,9},{9,8},{10,11... | collective-permute-start | bytes 1966088 | tf_op jit(solution)/shard_map/ppermute | solution.py:411
  43.9 2.3 %collective-permute-start.11 = (bf16[8,68,128]{2,1,0:T(8,128)(2,1)S(1)}, bf16[8,68,128]{2,1,0:T(8,128)(2,1)S(1)}, u32[]{:S(2)}, u32[]{:S(2)}) collective-permute-start(bf16[8,68,128]{2,1,0:T(8,128)(2,1)S(1)} %get-tuple-element.37), channel_id=1, source_target_pairs={{0,1},{1,0},{2,3},{3,2},{4,5},{5,4},{6,7},{7,6},{8,9},{9,8},{10,11... | collective-permute-start | bytes 417800 | tf_op jit(solution)/shard_map/ppermute | solution.py:412
  46.7 10.4 %collective-permute-start.12 = (bf16[296,128]{1,0:T(8,128)(2,1)S(1)}, bf16[296,128]{1,0:T(8,128)(2,1)S(1)}, u32[]{:S(2)}, u32[]{:S(2)}) collective-permute-start(bf16[296,128]{1,0:T(8,128)(2,1)S(1)} %get-tuple-element.39), channel_id=1, source_target_pairs={{0,14},{1,15},{2,12},{3,13},{4,10},{5,11},{6,8},{7,9},{8,6},{9,7},... | collective-permute-start | bytes 227336 | tf_op jit(solution)/shard_map/ppermute | solution.py:67
  51.7 9.9 %collective-permute-start.13 = (bf16[296,128]{1,0:T(8,128)(2,1)S(1)}, bf16[296,128]{1,0:T(8,128)(2,1)S(1)}, u32[]{:S(2)}, u32[]{:S(2)}) collective-permute-start(bf16[296,128]{1,0:T(8,128)(2,1)S(1)} %get-tuple-element.40), channel_id=1, source_target_pairs={{0,12},{1,13},{2,14},{3,15},{4,8},{5,9},{6,10},{7,11},{8,4},{9,5},... | collective-permute-start | bytes 227336 | tf_op jit(solution)/shard_map/ppermute | solution.py:67
  51.8 12.4 %collective-permute-start.14 = (bf16[296,128]{1,0:T(8,128)(2,1)S(1)}, bf16[296,128]{1,0:T(8,128)(2,1)S(1)}, u32[]{:S(2)}, u32[]{:S(2)}) collective-permute-start(bf16[296,128]{1,0:T(8,128)(2,1)S(1)} %get-tuple-element.41), channel_id=1, source_target_pairs={{0,10},{1,11},{2,8},{3,9},{4,14},{5,15},{6,12},{7,13},{8,2},{9,3},... | collective-permute-start | bytes 227336 | tf_op jit(solution)/shard_map/ppermute | solution.py:67
  54.2 11.6 %collective-permute-start.15 = (bf16[296,128]{1,0:T(8,128)(2,1)S(1)}, bf16[296,128]{1,0:T(8,128)(2,1)S(1)}, u32[]{:S(2)}, u32[]{:S(2)}) collective-permute-start(bf16[296,128]{1,0:T(8,128)(2,1)S(1)} %get-tuple-element.42), channel_id=1, source_target_pairs={{0,8},{1,9},{2,10},{3,11},{4,12},{5,13},{6,14},{7,15},{8,0},{9,1},... | collective-permute-start | bytes 227336 | tf_op jit(solution)/shard_map/ppermute | solution.py:67
  55.5 10.3 %collective-permute-start.16 = (bf16[296,128]{1,0:T(8,128)(2,1)S(1)}, bf16[296,128]{1,0:T(8,128)(2,1)S(1)}, u32[]{:S(2)}, u32[]{:S(2)}) collective-permute-start(bf16[296,128]{1,0:T(8,128)(2,1)S(1)} %get-tuple-element.43), channel_id=1, source_target_pairs={{0,6},{1,7},{2,4},{3,5},{4,2},{5,3},{6,0},{7,1},{8,14},{9,15},{10,... | collective-permute-start | bytes 227336 | tf_op jit(solution)/shard_map/ppermute | solution.py:67
  57.0 9.5 %collective-permute-start.17 = (bf16[296,128]{1,0:T(8,128)(2,1)S(1)}, bf16[296,128]{1,0:T(8,128)(2,1)S(1)}, u32[]{:S(2)}, u32[]{:S(2)}) collective-permute-start(bf16[296,128]{1,0:T(8,128)(2,1)S(1)} %get-tuple-element.44), channel_id=1, source_target_pairs={{0,4},{1,5},{2,6},{3,7},{4,0},{5,1},{6,2},{7,3},{8,12},{9,13},{10,... | collective-permute-start | bytes 227336 | tf_op jit(solution)/shard_map/ppermute | solution.py:67
  61.6 4.9 %collective-permute-start.18 = (bf16[296,128]{1,0:T(8,128)(2,1)S(1)}, bf16[296,128]{1,0:T(8,128)(2,1)S(1)}, u32[]{:S(2)}, u32[]{:S(2)}) collective-permute-start(bf16[296,128]{1,0:T(8,128)(2,1)S(1)} %get-tuple-element.45), channel_id=1, source_target_pairs={{0,2},{1,3},{2,0},{3,1},{4,6},{5,7},{6,4},{7,5},{8,10},{9,11},{10,... | collective-permute-start | bytes 227336 | tf_op jit(solution)/shard_map/ppermute | solution.py:67
